TPU v7x, 128 devices: a whole 4x4x4 slice. The times are simulated.
128 devices in a mesh: row: 4 (over x_hi, core), col: 32 (over z, y, x_lo).
Axes of the slice: x: 4 (x_hi: 2, x_lo: 2; x = x_hi * 2 + x_lo), y: 4, z: 4, core: 2. Of those that a mesh axis runs over, the one named last changes fastest.
Arguments:
- rows: bfloat16 [4096, 4096], P(('row', 'col')), may hold values from -6 to 6
- task_ids: int32 [4096], P(('row', 'col')), may hold values from 0 to 8, as said below
- task_embed: bfloat16 [8, 4096], replicated, may hold values from -6 to 6
- norm_gain: float32 [4, 4096], replicated, may hold values from 0.1 to 1.9
- layer_weight: bfloat16 [4, 4096, 4096], P(None, None, 'col'), may hold values from -0.09375 to 0.09375
Outputs:
- packed_out: bfloat16 [4096, 4096], P('row', 'col')
Inputs may be any that keep to these rules, and one draw needn't show every extreme that they name: `task_ids`: 8 marks an empty row, smaller values name a task.
All inputs are finite; a program needn't handle non-finite values.
Results may differ from a plain program's by a relative error of at most 0.008.
Values may be sent and summed in bfloat16 or wider, within the bound.
A program may use at most 128 MiB of HBM per device.

v0:
```python
import jax
import jax.numpy as jnp
from jax import lax
from jax.sharding import Mesh
from jax.sharding import PartitionSpec as P

COL = ("col_0", "col_1", "col_2")
ROW_COL = ("row", "col_0", "col_1", "col_2")


epsilon = 1e-06


def from_everyone(x, axis):
    size = lax.axis_size(axis)
    return lax.all_to_all(jnp.broadcast_to(x[None], (size, *x.shape)), axis, 0, 0, tiled=True)


def folded_in_pairs(pieces, combine):
    while len(jax.tree.leaves(pieces)[0]) > 1:
        pieces = jax.vmap(combine)(*(pieces[side::2] for side in (0, 1)))
    return pieces[0]


def entering(x, axis, combine, identity):
    size, index = (lax.axis_size(axis), lax.axis_index(axis))
    passed = jnp.arange(size) < index

    def kept(part, zero, own):
        part = jnp.where(
            passed.reshape(-1, *(1 for _ in own.shape)), part, jnp.asarray(zero, own.dtype)
        )
        return part

    pieces = from_everyone(x, axis)
    return folded_in_pairs(kept(pieces, identity, x), combine)


def taken_together(x, axis):
    return from_everyone(x, axis).sum(axis=0)


def rows_for(lines, size):
    spare = -len(lines) % size
    return jnp.pad(lines, [(0, spare)] + [(0, 0)] * (lines.ndim - 1))


def own_block(blocks, axes, turns):
    dims = [lax.axis_size(a) for a in axes]
    blocks = blocks.reshape(*dims, *blocks.shape[1:])
    blocks = blocks.transpose(*turns, *range(len(axes), blocks.ndim))
    blocks = blocks.reshape(-1, *blocks.shape[len(axes) :])
    for k in turns:
        blocks = lax.psum_scatter(blocks, axes[k], scatter_dimension=0, tiled=True)
    return blocks[0]


def all_blocks(x, axes, turns):
    blocks = x
    for k in turns:
        blocks = lax.all_gather(blocks, axes[k])
    done = turns[::-1]
    back = [done.index(k) for k in range(len(axes))]
    blocks = blocks.transpose(*back, *range(len(axes), blocks.ndim))
    return blocks.reshape(-1, *x.shape)


def total_of(x, axes, turns):
    size, lines = (lax.axis_size(axes), x.reshape(-1, *x.shape[1:][-1:]))
    blocks = rows_for(lines, size).reshape(size, -1, *lines.shape[1:])
    own = own_block(blocks, axes, turns)
    whole = all_blocks(own, axes, turns[::-1]).reshape(-1, *lines.shape[1:])
    return whole[: len(lines)].reshape(x.shape)


def add_counts(earlier, later):
    return earlier + later


def activate_rows(hidden, gain):
    total_rows = hidden.shape[0]
    width = hidden.shape[1]
    block_rows = min(512, total_rows)

    def one_block(block):
        values = block.astype(jnp.float32)
        inverse_rms = lax.rsqrt(jnp.mean(values * values, axis=1, keepdims=True) + epsilon)
        return jax.nn.silu(values * inverse_rms * gain[None, :]).astype(jnp.bfloat16)

    blocks = hidden.reshape(total_rows // block_rows, block_rows, width)
    return lax.map(one_block, blocks).reshape(total_rows, width)


def shards(rows, task_ids, task_embed, norm_gain, layer_weight):
    row_count = rows.shape[0]
    width = rows.shape[1]
    task_count = task_embed.shape[0]
    row_devices = lax.axis_size("row")
    col_devices = lax.axis_size(COL)
    capacity = row_count // row_devices + task_count
    slots_group = row_count * col_devices
    task_range = jnp.arange(task_count, dtype=jnp.int32)
    member = (task_ids[:, None] == task_range[None, :]).astype(jnp.int32)
    counts = jnp.sum(member, axis=0)
    zero_counts = jnp.zeros_like(counts)
    before_col = entering(counts, COL, add_counts, zero_counts)
    row_total = taken_together(counts, COL)
    before_row = entering(row_total, "row", add_counts, zero_counts)
    totals = taken_together(row_total, "row")
    before = before_row + before_col
    task_base = jnp.cumsum(totals) - totals
    positions = jnp.arange(row_count, dtype=jnp.int32)
    earlier_mask = positions[None, :] < positions[:, None]
    same_task = task_ids[:, None] == task_ids[None, :]
    task_rank = jnp.sum((same_task & earlier_mask).astype(jnp.int32), axis=1)
    row_live = task_ids < task_count
    packed_pos = (
        jnp.sum(member * (task_base + before)[None, :], axis=1).astype(jnp.int32) + task_rank
    )
    target_row = packed_pos % row_devices
    slot_index = packed_pos // row_devices
    before_pos = packed_pos[None, :] < packed_pos[:, None]
    same_target = (target_row[:, None] == target_row[None, :]) & row_live[None, :]
    within = jnp.sum((same_target & before_pos).astype(jnp.int32), axis=1)
    send_at = jnp.where(row_live, target_row * capacity + within, -1)
    buffer_range = jnp.arange(row_devices * capacity, dtype=jnp.int32)
    select = buffer_range[:, None] == send_at[None, :]
    send_rows = jnp.dot(
        select.astype(jnp.bfloat16), rows, preferred_element_type=jnp.float32
    ).astype(jnp.bfloat16)
    send_rows = send_rows.reshape(row_devices, capacity, width)
    send_slots = jnp.sum(jnp.where(select, slot_index[None, :] + 1, 0), axis=1) - 1
    send_slots = send_slots.reshape(row_devices, capacity)
    got_rows, got_slots = (
        lax.all_to_all(send_rows, "row", split_axis=0, concat_axis=0, tiled=True),
        lax.all_to_all(send_slots, "row", split_axis=0, concat_axis=0, tiled=True),
    )
    got_rows = got_rows.reshape(row_devices * capacity, width)
    got_slots = got_slots.reshape(row_devices * capacity)
    slot_range = jnp.arange(slots_group, dtype=jnp.int32)
    placing = (slot_range[:, None] == got_slots[None, :]).astype(jnp.bfloat16)
    local_part = jnp.dot(placing, got_rows, preferred_element_type=jnp.float32).astype(jnp.bfloat16)
    placed = total_of(local_part, COL, (0, 1, 2)).astype(jnp.float32)
    group_index = lax.axis_index("row")
    slot_pos = slot_range * row_devices + group_index
    in_task = (slot_pos[:, None] >= task_base[None, :]) & (
        slot_pos[:, None] < (task_base + totals)[None, :]
    )
    task_term = jnp.dot(
        in_task.astype(jnp.bfloat16), task_embed, preferred_element_type=jnp.float32
    )
    hidden = (placed + task_term).astype(jnp.bfloat16)
    part_width = width // col_devices
    column = lax.axis_index(COL) * part_width
    layers = layer_weight.shape[0]
    result = hidden
    for layer_index in range(layers):
        active = activate_rows(hidden, norm_gain[layer_index])
        update = jnp.dot(active, layer_weight[layer_index], preferred_element_type=jnp.float32)
        own_cols = lax.dynamic_slice_in_dim(hidden, column, part_width, 1).astype(jnp.float32)
        result = (own_cols + update).astype(jnp.bfloat16)
        if layer_index + 1 < layers:
            hidden = lax.all_gather(result, COL, axis=1, tiled=True)
    return result


def solution(mesh):
    finer = Mesh(
        mesh.devices.reshape(mesh.shape["row"], 4, 4, 2), ("row", "col_0", "col_1", "col_2")
    )
    return jax.shard_map(
        shards,
        mesh=finer,
        in_specs=(P(ROW_COL, None), P(ROW_COL), P(), P(), P(None, None, COL)),
        out_specs=P("row", COL),
        check_vma=False,
    )
```

profile of v0, /device:TPU:1, one launch (start us, length us, event | category | flops | bytes accessed | tf_op | source)
XLA Modules:
  0.0 1062.6 jit_solution(16607815354569057039)
XLA Ops:
  7.9 9.8 all-to-all-start
  25.7 6.1 all-to-all-start.1
  52.9 8.1 all-to-all-done.3
  66.6 76.3 %reduce-scatter.4.cloned.1.call-done = bf16[8,32,4096]{2,1,0:T(8,128)(2,1)} async-done(((bf16[32,32,4096]{2,1,0:T(8,128)(2,1)}), bf16[8,32,4096]{2,1,0:T(8,128)(2,1)}) %reduce-scatter.4.cloned.1.call-update) | async-done | bytes 2097168 | tf_op jit(solution)/shard_map/reduce_scatter | solution.py:54
  143.0 31.7 %reduce-scatter.6.cloned.1.call-done = bf16[2,32,4096]{2,1,0:T(8,128)(2,1)} async-done(((bf16[8,32,4096]{2,1,0:T(8,128)(2,1)}), bf16[2,32,4096]{2,1,0:T(8,128)(2,1)}) %reduce-scatter.6.cloned.1.call-update) | async-done | bytes 524304 | tf_op jit(solution)/shard_map/reduce_scatter | solution.py:54
  174.7 19.1 %reduce-scatter.8.cloned.1.call-done = bf16[1,32,4096]{2,1,0:T(8,128)(2,1)} async-done(((bf16[2,32,4096]{2,1,0:T(8,128)(2,1)}), bf16[1,32,4096]{2,1,0:T(8,128)(2,1)}) %reduce-scatter.8.cloned.1.call-update) | async-done | bytes 262160 | tf_op jit(solution)/shard_map/reduce_scatter | solution.py:54
  193.8 9.6 all_gather.24
  203.4 33.2 %all-gather.14.cloned.1.call-done = bf16[8,32,4096]{2,1,0:T(8,128)(2,1)} async-done(((bf16[2,32,4096]{2,1,0:T(8,128)(2,1)}), bf16[8,32,4096]{2,1,0:T(8,128)(2,1)}) %all-gather.14.cloned.1.call-update) | async-done | bytes 2097168 | tf_op jit(solution)/shard_map/all_gather | solution.py:61
  236.9 84.5 %all-gather.16.cloned.1.call-done = bf16[16,2,32,4096]{3,2,1,0:T(8,128)(2,1)} async-done(((bf16[4,2,32,4096]{3,2,1,0:T(8,128)(2,1)}), bf16[16,2,32,4096]{3,2,1,0:T(8,128)(2,1)}) %all-gather.16.cloned.1.call-update) | async-done | bytes 8388624 | tf_op jit(solution)/shard_map/all_gather | solution.py:61
  321.4 9.1 fusion.36
  334.7 17.3 %while.40 = (s32[]{:T(128)}, bf16[2,512,4096]{2,1,0:T(8,128)(2,1)}, bf16[2,512,4096]{2,1,0:T(8,128)(2,1)}, f32[1,4096]{1,0:T(1,128)S(1)}, s32[]{:T(128)}) while((s32[]{:T(128)}, bf16[2,512,4096]{2,1,0:T(8,128)(2,1)}, bf16[2,512,4096]{2,1,0:T(8,128)(2,1)}, f32[1,4096]{1,0:T(1,128)S(1)}, s32[]{:T(128)}) %tuple.89), condition=%wide.region_13.14_spmd, body=%wide.region_11.13_spmd.sunk | while | flops 23069184 | bytes 12608065 | solution.py:91
  346.5 5.6 fusion.78
  352.1 6.8 fusion.37
  359.1 194.6 %all-gather.8.cloned.1.call-done = bf16[1024,4096]{1,0:T(8,128)(2,1)} async-done(((bf16[1024,128]{1,0:T(8,128)(2,1)}), bf16[1024,4096]{1,0:T(8,128)(2,1)}) %all-gather.8.cloned.1.call-update) | async-done | bytes 8388624 | tf_op jit(solution)/shard_map/all_gather | solution.py:163
  558.0 17.3 %while.41 = (s32[]{:T(128)}, bf16[2,512,4096]{2,1,0:T(8,128)(2,1)}, bf16[2,512,4096]{2,1,0:T(8,128)(2,1)}, f32[1,4096]{1,0:T(1,128)S(1)}, s32[]{:T(128)}) while((s32[]{:T(128)}, bf16[2,512,4096]{2,1,0:T(8,128)(2,1)}, bf16[2,512,4096]{2,1,0:T(8,128)(2,1)}, f32[1,4096]{1,0:T(1,128)S(1)}, s32[]{:T(128)}) %tuple.91), condition=%wide.region_16.17_spmd, body=%wide.region_14.16_spmd.sunk | while | flops 23069184 | bytes 12608065 | solution.py:91
  575.3 6.8 fusion.38
  582.4 208.1 %all-gather.10.cloned.1.call-done = bf16[1024,4096]{1,0:T(8,128)(2,1)} async-done(((bf16[1024,128]{1,0:T(8,128)(2,1)}), bf16[1024,4096]{1,0:T(8,128)(2,1)}) %all-gather.10.cloned.1.call-update) | async-done | bytes 8388624 | tf_op jit(solution)/shard_map/all_gather | solution.py:163
  794.8 17.3 %while.42 = (s32[]{:T(128)}, bf16[2,512,4096]{2,1,0:T(8,128)(2,1)}, bf16[2,512,4096]{2,1,0:T(8,128)(2,1)}, f32[1,4096]{1,0:T(1,128)S(1)}, s32[]{:T(128)}) while((s32[]{:T(128)}, bf16[2,512,4096]{2,1,0:T(8,128)(2,1)}, bf16[2,512,4096]{2,1,0:T(8,128)(2,1)}, f32[1,4096]{1,0:T(1,128)S(1)}, s32[]{:T(128)}) %tuple.92), condition=%wide.region_19.20_spmd, body=%wide.region_17.19_spmd.sunk | while | flops 23069184 | bytes 12608065 | solution.py:91
  806.5 5.6 fusion.82
  812.1 6.8 fusion.39
  818.9 208.4 %all-gather.12.cloned.1.call-done = bf16[1024,4096]{1,0:T(8,128)(2,1)} async-done(((bf16[1024,128]{1,0:T(8,128)(2,1)}), bf16[1024,4096]{1,0:T(8,128)(2,1)}) %all-gather.12.cloned.1.call-update) | async-done | bytes 8388624 | tf_op jit(solution)/shard_map/all_gather | solution.py:163
  1031.6 17.3 %while.43 = (s32[]{:T(128)}, bf16[2,512,4096]{2,1,0:T(8,128)(2,1)}, bf16[2,512,4096]{2,1,0:T(8,128)(2,1)}, f32[1,4096]{1,0:T(1,128)S(1)}, s32[]{:T(128)}) while((s32[]{:T(128)}, bf16[2,512,4096]{2,1,0:T(8,128)(2,1)}, bf16[2,512,4096]{2,1,0:T(8,128)(2,1)}, f32[1,4096]{1,0:T(1,128)S(1)}, s32[]{:T(128)}) %tuple.90), condition=%wide.region_22.23_spmd, body=%wide.region_20.22_spmd.sunk | while | flops 23069184 | bytes 12608065 | solution.py:91
  1043.3 5.6 fusion.84
  1048.9 6.8 fusion.40
  (98 shorter events, 106.7 us)
Async XLA Ops:
  6.5 36.5 %copy-start = (bf16[32,4096]{1,0:T(8,128)(2,1)S(1)}, bf16[32,4096]{1,0:T(8,128)(2,1)}, u32[]{:S(2)}) copy-start(bf16[32,4096]{1,0:T(8,128)(2,1)} %param.13) | copy-start | bytes 786436
  7.9 16.8 %all-to-all-start = ((s32[32,1,8]{2,1,0:T(1,128)}), s32[32,1,8]{2,1,0:T(1,128)S(1)}, u32[]{:S(2)}, u32[]{:S(2)}) async-start(s32[32,1,8]{2,1,0:T(1,128)} %broadcast_in_dim.43), calls=%async_computation | async-start | bytes 32768 | tf_op jit(solution)/shard_map/all_to_all | solution.py:16
  25.7 10.6 all-to-all-start.1
  39.1 8.4 all-to-all-start.2
  47.5 13.5 %all-to-all-start.3 = ((bf16[4,16,4096]{2,1,0:T(8,128)(2,1)}), bf16[4,16,4096]{2,1,0:T(8,128)(2,1)S(1)}, u32[]{:S(2)}, u32[]{:S(2)}) async-start(bf16[4,16,4096]{2,1,0:T(8,128)(2,1)} %bitcast.11), calls=%async_computation.3 | async-start | bytes 1048576 | tf_op jit(solution)/shard_map/all_to_all | solution.py:135
  51.7 91.2 %reduce-scatter.4.cloned.1.call-start = ((), (), s32[]{:S(2)}) async-start(), calls=%async_computation.7 | async-start | bytes 10485760 | tf_op jit(solution)/shard_map/reduce_scatter | solution.py:54
  66.6 170.3 %copy-start.3 = (f32[4,4096]{1,0:T(4,128)S(1)}, f32[4,4096]{1,0:T(4,128)}, u32[]{:S(2)}) copy-start(f32[4,4096]{1,0:T(4,128)} %param.16) | copy-start | bytes 196612
  66.6 254.9 %copy-start.2 = (bf16[8,4096]{1,0:T(8,128)(2,1)S(1)}, bf16[8,4096]{1,0:T(8,128)(2,1)}, u32[]{:S(2)}) copy-start(bf16[8,4096]{1,0:T(8,128)(2,1)} %param.15) | copy-start | bytes 196612
  66.6 108.0 %reduce-scatter.6.cloned.1.call-start = ((), (), s32[]{:S(2)}) async-start(), calls=%async_computation.8 | async-start | bytes 2621440 | tf_op jit(solution)/shard_map/reduce_scatter | solution.py:54
  142.9 50.8 %reduce-scatter.8.cloned.1.call-start = ((), (), s32[]{:S(2)}) async-start(), calls=%async_computation.9 | async-start | bytes 786432 | tf_op jit(solution)/shard_map/reduce_scatter | solution.py:54
  174.7 61.9 %all-gather.14.cloned.1.call-start = ((), (), s32[]{:S(2)}) async-start(), calls=%async_computation.13 | async-start | bytes 2621440 | tf_op jit(solution)/shard_map/all_gather | solution.py:61
  203.3 118.1 %all-gather.16.cloned.1.call-start = ((), (), s32[]{:S(2)}) async-start(), calls=%async_computation.14 | async-start | bytes 10485760 | tf_op jit(solution)/shard_map/all_gather | solution.py:61
  236.6 317.1 %all-gather.8.cloned.1.call-start = ((), (), s32[]{:S(2)}) async-start(), calls=%async_computation.10 | async-start | bytes 8650752 | tf_op jit(solution)/shard_map/all_gather | solution.py:163
  358.9 431.7 %all-gather.10.cloned.1.call-start = ((), (), s32[]{:S(2)}) async-start(), calls=%async_computation.11 | async-start | bytes 8650752 | tf_op jit(solution)/shard_map/all_gather | solution.py:163
  582.1 445.2 %all-gather.12.cloned.1.call-start = ((), (), s32[]{:S(2)}) async-start(), calls=%async_computation.12 | async-start | bytes 8650752 | tf_op jit(solution)/shard_map/all_gather | solution.py:163
  1048.9 6.8 copy-start.1
Sparse Core Ops, SparseCore 0:
  66.7 76.1 reduce-scatter.3
  145.3 29.2 reduce-scatter.5
  177.0 16.7 reduce-scatter.7
  203.5 33.0 all-gather.13
  238.1 83.2 all-gather.15
  359.0 194.7 all-gather.7
  582.3 208.2 all-gather.9
  819.0 208.2 all-gather.11
where the time goes:
time: 1080 us; the launch traced here: 1060 us
  waiting for transfers between devices  877 us (81%)
  other arithmetic  74.6 us (7%)
  matrix products  42.9 us (4%)
  starting transfers between devices  24.9 us (2%)
  local copies, waits for them, and re-layouts  19.8 us (2%)
  between operations  13.6 us (1%)
    all_gather x3, waiting for transfers between devices, shards(): hidden = lax.all_gather(result, COL, axis=1, tiled=True)  611 us
    reduce_scatter x3, waiting for transfers between devices, own_block(): blocks = lax.psum_scatter(blocks, axes[k], scatter_dimension=0, tiled=True)  127 us
    all_gather x2, waiting for transfers between devices, all_blocks(): blocks = lax.all_gather(blocks, axes[k])  118 us
    dynamic_update_slice x8, other arithmetic, activate_rows(): return lax.map(one_block, blocks).reshape(total_rows, width)  44.6 us
    dot_general x4, matrix products, shards(): jnp.dot(active, layer_weight[layer_index], preferred_element_type=jnp.flo...  27.1 us
    reduce_sum x8, other arithmetic, one_block(): jnp.mean(values * values, axis=1, keepdims=True) + epsilon  24.6 us
  transfers between devices with their start and end apart: 12, of which 12 were waited for; matrix products, arithmetic and copies ran while one was open for 0% of the time, Pallas kernels for 0%

commit v1 on v0

v1 whole, which is shorter than its diff:
```python
import functools

import jax
import jax.numpy as jnp
from jax import lax
from jax.experimental import pallas as pl
from jax.experimental.pallas import tpu as pltpu
from jax.sharding import PartitionSpec as P

MESH = pl.DeviceIdType.MESH
F32 = jnp.float32
BF16 = jnp.bfloat16
EPS = 1e-06
LAYERS = 4
CUBE = [(1, 0, 0), (0, 1, 0), (0, 0, 1), (1, 1, 0), (0, 1, 1), (1, 0, 1), (1, 1, 1)]
NEXT = (1, 2, 0)
PREV = (2, 0, 1)
THIRDS = ((0, 3), (3, 3), (6, 2))
FAR = [(i // 4, (i // 2) % 2, i % 2) for i in range(1, 8)]


def flip(bit, on):
    return 1 - bit if on else bit


def kernel(
    rows_ref, ids_ref, embed_ref, gain_ref, w_ref, out_ref,
    wv, a, act, acc, h0s, h0, gp, pm, f, idg, idf, pos, stat, invb, oacc,
    wl, ws1s, ws1r, ws2s, ws2r, wds, wdr, a1s, a1r, a2s, a2r, a3s, a3r,
    hs, hr, i1s, i1r, i2s, i2r, i3s, i3r, sts, str_, fs, fr, fds, fdr,
):
    row, col = lax.axis_index("row"), lax.axis_index("col")
    xh, core = row // 2, row % 2
    z, y, x = col // 8, (col // 2) % 4, col % 2
    zh, zo, yh, yo = z // 2, z % 2, y // 2, y % 2
    zl, yl = zo + zh - 2 * zo * zh, yo + yh - 2 * yo * yh
    qme = zl * 4 + yl * 2 + x

    def cube_dev(fl):
        return (row, (zh * 2 + flip(zo, fl[2])) * 8 + (yh * 2 + flip(yo, fl[1])) * 2 + flip(x, fl[0]))

    def cube_q(fl):
        return flip(zl, fl[2]) * 4 + flip(yl, fl[1]) * 2 + flip(x, fl[0])

    def far_dev(fl):
        zz = 3 - z if fl[1] else z
        yy = 3 - y if fl[2] else y
        return (flip(xh, fl[0]) * 2 + core, zz * 8 + yy * 2 + x)

    def slot(fa, fb):
        return flip(zh, fa) * 2 + flip(yh, fb)

    def cols(s):
        return pl.ds(pl.multiple_of(s * 128, 128), 128)

    partner = (xh * 2 + (1 - core), col)
    links = [cube_dev(CUBE[d]) for d in range(3)]
    wlinks = [far_dev((0, 0, 1)), far_dev((0, 1, 0))]

    def remote(src, dst, ss, rs, dev):
        return pltpu.make_async_remote_copy(
            src_ref=src, dst_ref=dst, send_sem=ss, recv_sem=rs, device_id=dev, device_id_type=MESH
        )

    def both(ref, ss, rs, dev):
        return remote(ref, ref, ss, rs, dev)

    def load_own(l):
        for zz in range(4):
            for yy in range(4):
                q0 = min(zz, 3 - zz) * 4 + min(yy, 3 - yy) * 2
                pltpu.make_async_copy(
                    w_ref.at[l, zz, yy],
                    wv.at[l, pl.ds(q0, 2), (zz // 2) * 2 + yy // 2, :, cols(slot(0, 0))],
                    wl.at[l],
                ).start()

    def own_loaded(l):
        whole = wv.at[l, :, :, :, cols(slot(0, 0))]
        pltpu.make_async_copy(whole, whole, wl.at[l]).wait()

    def wpart(l, fa, fb, q0, n):
        return wv.at[l, pl.ds(q0, n), :, :, cols(slot(fa, fb))]

    def w1(l, k, j, recv=False):
        fa, fb = ((0, 1) if k == 0 else (1, 0)) if recv else (0, 0)
        return both(wpart(l, fa, fb, core * 4 + 2 * j, 2), ws1s.at[l, k, j], ws1r.at[l, k, j], wlinks[k])

    def w2(l, k, recv=False):
        fa, fb = (1, 1) if recv else ((1, 0) if k == 0 else (0, 1))
        return both(wpart(l, fa, fb, core * 4 + 2 * (1 - k), 2), ws2s.at[l, k], ws2r.at[l, k], wlinks[k])

    def wd(l, k, recv=False):
        fa, fb = ((0, 1), (1, 0), (1, 1))[k]
        half = (1 - core) if recv else core
        return both(wpart(l, fa, fb, half * 4, 4), wds.at[l, k], wdr.at[l, k], partner)

    def w1_send(l):
        own_loaded(l)
        for k, j in ((0, 0), (1, 1), (0, 1), (1, 0)):
            w1(l, k, j).start()

    def w1_first(l):
        w1(l, 0, 0, True).wait_recv()
        w1(l, 1, 1, True).wait_recv()
        w2(l, 1).start()
        w2(l, 0).start()

    def w1_rest(l):
        w1(l, 0, 1, True).wait_recv()
        wd(l, 0).start()
        w1(l, 1, 0, True).wait_recv()
        wd(l, 1).start()

    def w2_in(l):
        w2(l, 0, True).wait_recv()
        w2(l, 1, True).wait_recv()
        wd(l, 2).start()

    def wd_in(l):
        for k in range(3):
            wd(l, k, True).wait_recv()

    def zero(l):
        return isinstance(l, int)

    def chunk(l, fl, i):
        if zero(l):
            at = pl.ds(pl.multiple_of(flip(yo, fl[1]) * 64 + flip(x, fl[0]) * 32, 32), 32)
            return a.at[0, pl.ds(4 * i, 4), flip(zo, fl[2]), at, :]
        return a.at[l, cube_q(fl), i]

    def third(l, fl, e):
        if zero(l):
            at = pl.ds(pl.multiple_of(flip(yo, fl[1]) * 64 + flip(x, fl[0]) * 32, 32), 32)
            return a.at[0, pl.ds(*THIRDS[e]), flip(zo, fl[2]), at, :]
        if e == 2:
            return a.at[l, cube_q(fl), :, pl.ds(80, 48), :]
        return a.at[l, cube_q(fl), e, pl.ds(0, 80), :]

    ME, ALL = (0, 0, 0), (1, 1, 1)

    def pair(d):
        e = PREV[d]
        return tuple(int(k in (d, e)) for k in range(3))

    def s1(l, d, i, recv=False):
        return both(chunk(l, CUBE[d] if recv else ME, i), a1s.at[l, d, i], a1r.at[l, d, i], links[d])

    def s2(l, d, i, recv=False):
        return both(chunk(l, pair(d) if recv else CUBE[PREV[d]], i), a2s.at[l, d, i], a2r.at[l, d, i], links[d])

    def s3(l, d, recv=False):
        return both(third(l, ALL if recv else pair(PREV[d]), d), a3s.at[l, d], a3r.at[l, d], links[d])

    def step1(l):
        for i in range(2):
            for d in range(3):
                s1(l, d, i).start()

    def step2(l, i):
        for d in range(3):
            s1(l, d, i, True).wait_recv()
        for d in range(3):
            s2(l, d, i).start()

    def step3(l):
        for i in range(2):
            for d in range(3):
                s2(l, d, i, True).wait_recv()
        for d in range(3):
            s3(l, d).start()

    def step3_in(l):
        for d in range(3):
            s3(l, d, True).wait_recv()

    def stat_copy(l, k, recv=False):
        q = cube_q(CUBE[k]) if recv else qme
        return both(stat.at[l, q], sts.at[l, k], str_.at[l, k], cube_dev(CUBE[k]))

    def eye():
        return lax.broadcasted_iota(jnp.int32, (256, 256), 0) == lax.broadcasted_iota(jnp.int32, (256, 256), 1)

    def multiply(l, src, held):
        acc[...] = held.reshape(256, 512).astype(F32)

        def body(q, carry):
            acc[...] += jnp.dot(src(q), wv[l, q].reshape(512, 512), preferred_element_type=F32)
            return carry

        lax.fori_loop(0, 8, body, 0)
        new = acc[...].astype(BF16)
        a[l + 1, qme] = new.reshape(2, 128, 512)
        val = new.astype(F32)
        sq = val * val
        sq = (sq[:, 0:128] + sq[:, 128:256]) + (sq[:, 256:384] + sq[:, 384:512])
        total = jnp.sum(sq, axis=1, keepdims=True)
        line = jnp.sum(jnp.where(eye(), total, 0.0), axis=0, keepdims=True)
        stat[l + 1, qme] = jnp.broadcast_to(line, (8, 256))

    def read_stats(l):
        total = stat[l, 0]
        for q in range(1, 8):
            total = total + stat[l, q]
        half = 0.5 * lax.rsqrt(total[0:1] * (1.0 / 4096.0) + EPS)
        tall = jnp.sum(jnp.where(eye(), half, 0.0), axis=1, keepdims=True)
        invb[...] = jnp.broadcast_to(tall, (256, 128))

    def activate(l, q):
        for t in range(4):
            c = slice(t * 128, t * 128 + 128)
            u = a[l, q, :, :, c].reshape(256, 128).astype(F32) * invb[...] * gp[l, q, 0:1, c]
            act[q, :, c] = (u + u * jnp.tanh(u)).astype(BF16)

    def h_copy(k, recv=False):
        fl = CUBE[k] if recv else ME
        dst = h0.at[flip(zo, fl[2]), pl.ds(pl.multiple_of(flip(yo, fl[1]) * 64 + flip(x, fl[0]) * 32, 32), 32), :]
        src = dst if recv else h0s.at[cube_q(CUBE[k])]
        return remote(src, dst, hs.at[k], hr.at[k], cube_dev(CUBE[k]))

    def id1(k, recv=False):
        fl = CUBE[k] if recv else ME
        return both(
            idg.at[flip(zo, fl[2]), flip(yo, fl[1]) * 2 + flip(x, fl[0])], i1s.at[k], i1r.at[k], cube_dev(CUBE[k])
        )

    def far_at(fl):
        return (flip(xh, fl[0]) * 2 + core) * 2 + flip(zh, fl[1]), flip(yh, fl[2])

    def id2(k, recv=False):
        g, b = far_at(FAR[k] if recv else ME)
        dst = idf.at[g, :, b]
        return remote(dst if recv else idg, dst, i2s.at[k], i2r.at[k], far_dev(FAR[k]))

    def id3(k, recv=False):
        c = (1 - core) if recv else core
        return both(idf.at[pl.ds((k * 2 + c) * 2, 2)], i3s.at[k], i3r.at[k], partner)

    def out1(k, recv=False):
        g, b = far_at(FAR[k] if recv else ME)
        dst = f.at[g, :, b]
        src = dst if recv else a.at[LAYERS, qme, :, :, cols(slot(FAR[k][1], FAR[k][2]))]
        return remote(src, dst, fs.at[k], fr.at[k], far_dev(FAR[k]))

    def out2(k, recv=False):
        fl = ([ME] + FAR)[k]
        c = (1 - core) if recv else core
        g = (flip(xh, fl[0]) * 2 + c) * 2 + flip(zh, fl[1])
        return both(f.at[g, :, flip(yh, fl[2])], fds.at[k], fdr.at[k], partner)

    def positions():
        spread = idf[...].reshape(1024, 128).astype(F32).astype(BF16)
        k = lax.broadcasted_iota(jnp.int32, (32, 1024), 0)
        j = lax.broadcasted_iota(jnp.int32, (32, 1024), 1)
        pick = jnp.where((j // 32 == k) & (j % 8 == 0), 1.0, 0.0).astype(BF16)
        code = jnp.dot(pick, spread, preferred_element_type=F32)
        member = jnp.concatenate([jnp.where(code == 8.0 - t, 1.0, 0.0) for t in range(8)], axis=0).astype(BF16)
        i0 = lax.broadcasted_iota(jnp.int32, (128, 128), 0)
        i1 = lax.broadcasted_iota(jnp.int32, (128, 128), 1)
        upper = jnp.where(i0 < i1, 1.0, 0.0).astype(BF16)
        within = jnp.dot(member, upper, preferred_element_type=F32)
        count = jnp.dot(member, jnp.ones((128, 128), BF16), preferred_element_type=F32).astype(BF16)
        j0 = lax.broadcasted_iota(jnp.int32, (256, 256), 0)
        j1 = lax.broadcasted_iota(jnp.int32, (256, 256), 1)
        lower = jnp.where(j1 < j0, 1.0, 0.0).astype(BF16)
        place = jnp.dot(lower, count, preferred_element_type=F32) + within
        where = jnp.full((32, 128), -1.0, F32)
        for t in range(8):
            where = jnp.where(code == 8.0 - t, place[t * 32 : t * 32 + 32], where)
        for k in range(32):
            pos[k, 0:1, :] = where[k : k + 1]

    def selection(k0, k1):
        slots = (lax.broadcasted_iota(jnp.int32, (1024, 128), 0) * 4 + row).astype(F32)

        def body(k, carry):
            for half in range(2):
                hit = slots == pos[k * 2 + half, 0:1, :]
                pm[k, :, half * 128 : half * 128 + 128] = jnp.where(hit, 1.0, 0.0).astype(BF16)
            return carry

        lax.fori_loop(k0, k1, body, 0)

    for l in range(LAYERS):
        load_own(l)

    barrier = pltpu.get_barrier_semaphore()
    peers = [cube_dev(fl) for fl in CUBE] + [far_dev(fl) for fl in FAR] + [partner]
    for dev in peers:
        pl.semaphore_signal(barrier, inc=1, device_id=dev, device_id_type=MESH)
    pl.semaphore_wait(barrier, len(peers))

    w1_send(0)

    ids = 8.0 - ids_ref[...].astype(F32)
    i0 = lax.broadcasted_iota(jnp.int32, (32, 32), 0)
    i1 = lax.broadcasted_iota(jnp.int32, (32, 32), 1)
    code = jnp.sum(jnp.where(i0 == i1, ids, 0.0), axis=1, keepdims=True)
    own_rows = pl.ds(pl.multiple_of(yo * 64 + x * 32, 32), 32)
    square = jnp.zeros((32, 128), F32)
    tiles = [
        (q, s, ((q // 4 if s < 2 else 3 - q // 4) * 8 + ((q // 2) % 2 if s % 2 == 0 else 3 - (q // 2) % 2) * 2 + q % 2) * 128)
        for q in range(8)
        for s in range(4)
    ]
    for q, s, c in tiles:
        table = embed_ref[:, c : c + 128].astype(F32)
        term = jnp.zeros((32, 128), F32)
        for t in range(8):
            term = jnp.where(code == 8.0 - t, table[t : t + 1], term)
        start = (rows_ref[:, c : c + 128].astype(F32) + term).astype(BF16)
        h0s[q, :, s * 128 : s * 128 + 128] = start
        start = start.astype(F32)
        square = square + start * start
        for l in range(LAYERS):
            gp[l, q, 0:1, s * 128 : s * 128 + 128] = gain_ref[l : l + 1, c : c + 128]
    half = 0.5 * lax.rsqrt(jnp.sum(square, axis=1, keepdims=True) * (1.0 / 4096.0) + EPS)
    for q, s, c in tiles:
        lanes = slice(s * 128, s * 128 + 128)
        u = h0s[q, :, lanes].astype(F32) * half * gp[0, q, 0:1, lanes]
        a[0, q, zo, own_rows, lanes] = (u + u * jnp.tanh(u)).astype(BF16)
    step1(0)
    h0[zo, own_rows, :] = h0s[qme]
    for k in range(7):
        h_copy(k).start()
    lane = lax.broadcasted_iota(jnp.int32, (32, 128), 1)
    sub = lax.broadcasted_iota(jnp.int32, (32, 128), 0)
    line = jnp.sum(jnp.where(lane == sub + (col % 4) * 32, code, 0.0), axis=0, keepdims=True)
    idg[zo, yo * 2 + x] = jnp.broadcast_to(line, (8, 128)).astype(jnp.int32)
    for k in range(7):
        id1(k).start()

    step2(0, 0)
    w1_first(0)
    w1_send(1)
    step2(0, 1)
    for k in range(7):
        id1(k, True).wait_recv()
    g, b = far_at(ME)
    idf[g, :, b] = idg[...]
    for k in range(7):
        id2(k).start()
    for k in range(7):
        h_copy(k, True).wait_recv()
    step3(0)
    w1_rest(0)
    step3_in(0)
    w2_in(0)
    wd_in(0)
    multiply(0, lambda q: a[0, q].reshape(256, 512), h0[...])

    def layer(l, carry):
        for k in range(7):
            stat_copy(l, k).start()
        step1(l)
        w1_first(l)

        @pl.when(l < LAYERS - 1)
        def _():
            w1_send(l + 1)

        for k in range(7):
            stat_copy(l, k, True).wait_recv()
        read_stats(l)
        step2(l, 0)
        activate(l, qme)
        step2(l, 1)
        for d in range(3):
            activate(l, cube_q(CUBE[d]))
        w1_rest(l)
        step3(l)

        @pl.when(l == 1)
        def _():
            for k in range(7):
                id2(k, True).wait_recv()
            for k in range(2):
                id3(k).start()

        @pl.when(l == 2)
        def _():
            for k in range(2):
                id3(k, True).wait_recv()
            positions()

        @pl.when(l >= 2)
        def _():
            selection((l - 2) * 8, (l - 1) * 8)

        for d in range(3):
            activate(l, cube_q(pair(d)))
        w2_in(l)
        step3_in(l)
        activate(l, cube_q(ALL))
        wd_in(l)
        multiply(l, lambda q: act[q], a[l, qme])
        return carry

    lax.fori_loop(1, LAYERS, layer, 0)

    for k in range(7):
        out1(k).start()
    f[g, :, b] = a[LAYERS, qme, :, :, cols(slot(0, 0))]
    out2(0).start()
    for k in range(7):
        out1(k, True).wait_recv()
        out2(k + 1).start()
    for k in range(8):
        out2(k, True).wait_recv()
    oacc[...] = jnp.zeros_like(oacc)

    def place(k, carry):
        oacc[...] += jnp.dot(pm[k], f[k // 2, k % 2].reshape(256, 128), preferred_element_type=F32)
        return carry

    lax.fori_loop(0, 16, place, 0)
    out_ref[...] = oacc[...].astype(BF16)

    def drain(l, carry):
        for k in range(2):
            for j in range(2):
                w1(l, k, j).wait_send()
            w2(l, k).wait_send()
        for k in range(3):
            wd(l, k).wait_send()
        return carry

    lax.fori_loop(0, LAYERS, drain, 0)

    def drain_act(l):
        for d in range(3):
            for i in range(2):
                s1(l, d, i).wait_send()
                s2(l, d, i).wait_send()
            s3(l, d).wait_send()

    drain_act(0)

    def drain_layer(l, carry):
        drain_act(l)
        for k in range(7):
            stat_copy(l, k).wait_send()
        return carry

    lax.fori_loop(1, LAYERS, drain_layer, 0)
    for k in range(7):
        h_copy(k).wait_send()
        id1(k).wait_send()
        id2(k).wait_send()
        out1(k).wait_send()
    for k in range(2):
        id3(k).wait_send()
    for k in range(8):
        out2(k).wait_send()


def shards(rows, task_ids, task_embed, norm_gain, layer_weight):
    dma = pltpu.SemaphoreType.DMA
    vmem = pltpu.VMEM
    pairs = lambda *shape: [dma(shape), dma(shape)]
    return pl.pallas_call(
        kernel,
        out_shape=jax.ShapeDtypeStruct((1024, 128), BF16),
        in_specs=[pl.BlockSpec(memory_space=pltpu.VMEM)] * 4 + [pl.BlockSpec(memory_space=pl.ANY)],
        out_specs=pl.BlockSpec(memory_space=pltpu.VMEM),
        scratch_shapes=[
            vmem((4, 8, 4, 128, 512), BF16),
            vmem((5, 8, 2, 128, 512), BF16),
            vmem((8, 256, 512), BF16),
            vmem((256, 512), F32),
            vmem((8, 32, 512), BF16),
            vmem((2, 128, 512), BF16),
            vmem((4, 8, 8, 512), F32),
            vmem((16, 1024, 256), BF16),
            vmem((8, 2, 2, 128, 128), BF16),
            vmem((2, 4, 8, 128), jnp.int32),
            vmem((8, 2, 2, 4, 8, 128), jnp.int32),
            vmem((32, 8, 128), F32),
            vmem((5, 8, 8, 256), F32),
            vmem((256, 128), F32),
            vmem((1024, 128), F32),
            dma((4,)),
            *pairs(4, 2, 2),
            *pairs(4, 2),
            *pairs(4, 3),
            *pairs(4, 3, 2),
            *pairs(4, 3, 2),
            *pairs(4, 3),
            *pairs(7),
            *pairs(7),
            *pairs(7),
            *pairs(2),
            *pairs(4, 7),
            *pairs(7),
            *pairs(8),
        ],
        compiler_params=pltpu.CompilerParams(
            collective_id=0, has_side_effects=True, vmem_limit_bytes=60 * 1024 * 1024
        ),
    )(
        rows,
        task_ids.reshape(1, 32),
        task_embed,
        norm_gain,
        layer_weight.reshape(4, 4, 4, 2, 128, 128),
    )


def solution(mesh):
    return jax.shard_map(
        shards,
        mesh=mesh,
        in_specs=(P(("row", "col"), None), P(("row", "col")), P(), P(), P(None, None, "col")),
        out_specs=P("row", "col"),
        check_vma=False,
    )
```

time: 1080 us -> 118 us (0.11); the launches traced: 1060 us -> 117 us
  waiting for transfers between devices: 877 us -> 0 us
  Pallas kernels: 0 us -> 116 us
  other arithmetic: 74.6 us -> 0 us
  matrix products: 42.9 us -> 0 us
  starting transfers between devices: 24.9 us -> 0 us
  local copies, waits for them, and re-layouts: 19.8 us -> 1.67 us
  between operations: 13.6 us -> 0.01 us
    all_gather x5 -> x0, waiting for transfers between devices: 729 us -> none  [the longest x3 611 us: shards(): hidden = lax.all_gather(result, COL, axis=1, tiled=True)]
    reduce_scatter x3 -> x0, waiting for transfers between devices: 127 us -> none  [own_block(): blocks = lax.psum_scatter(blocks, axes[k], scatter_dimension=0, tiled=True)]
    pallas_call x0 -> x1, Pallas kernels: none -> 116 us  [shards(): pl.pallas_call(kernel, out_shape=jax.ShapeDtypeStruct((1024, 128), BF16),...]
    dynamic_update_slice x8 -> x0, other arithmetic: 44.6 us -> none  [activate_rows(): return lax.map(one_block, blocks).reshape(total_rows, width)]
    dot_general x7 -> x0, matrix products: 42.9 us -> none  [the longest x4 27.1 us: shards(): jnp.dot(active, layer_weight[layer_index], preferred_element_type=jnp.flo...]
    reduce_sum x15 -> x0, other arithmetic: 27.5 us -> none  [the longest x8 24.6 us: one_block(): jnp.mean(values * values, axis=1, keepdims=True) + epsilon]
    all_to_all x4 -> x0, starting transfers between devices: 23.9 us -> none  [the longest x2 15.9 us: from_everyone(): lax.all_to_all(jnp.broadcast_to(x[None], (size, *x.shape)), axis, 0, 0, t...]
    all_to_all x4 -> x0, waiting for transfers between devices: 21.4 us -> none  [the longest x2 9.96 us: from_everyone(): lax.all_to_all(jnp.broadcast_to(x[None], (size, *x.shape)), axis, 0, 0, t...]
  transfers between devices with their start and end apart: 12 -> 0, of which waited for: 12 -> 0; matrix products, arithmetic and copies ran while one was open for 0% -> 0% of each run, Pallas kernels for 0% -> 0%
where the time goes in v1:
time: 118 us; the launch traced here: 117 us
  Pallas kernels  116 us (98%)
  local copies, waits for them, and re-layouts  1.67 us (1%)
    pallas_call x1, Pallas kernels, shards(): pl.pallas_call(kernel, out_shape=jax.ShapeDtypeStruct((1024, 128), BF16),...  116 us

profile of v1, /device:TPU:1, one launch (start us, length us, event | category | flops | bytes accessed | tf_op | source)
XLA Modules:
  0.0 117.4 jit_solution(10450973222103678935)
XLA Ops:
  0.0 115.7 %shard_map.55 = bf16[1024,128]{1,0:T(8,128)(2,1)} custom-call(bf16[32,4096]{1,0:T(8,128)(2,1)} %rows_ref.1, s32[1,32]{1,0:T(1,128)} %bitcast.3, bf16[8,4096]{1,0:T(8,128)(2,1)} %embed_ref.1, f32[4,4096]{1,0:T(4,128)} %gain_ref.1, bf16[4,4,4,2,128,128]{5,4,3,2,1,0:T(8,128)(2,1)} %bitcast.2), custom_call_target="tpu_custom_call" | custom-call | tf_op jit(solution)/shard_map/pallas_call | solution.py:462
  115.7 1.7 %copy.7 = bf16[1024,128]{1,0:T(8,128)(2,1)} copy(bf16[1024,128]{1,0:T(8,128)(2,1)} %shard_map.55) | data formatting | bytes 524288

commit v2 on v1

--- a/solution.py
+++ b/solution.py
@@ -24,9 +24,10 @@
 
 
 def kernel(
-    rows_ref, ids_ref, embed_ref, gain_ref, w_ref, out_ref,
+    rows_in, ids_in, embed_in, gain_in, w_ref, out_ref,
+    rows_ref, ids_ref, embed_ref, gain_ref, outv,
     wv, a, act, acc, h0s, h0, gp, pm, f, idg, idf, pos, stat, invb, oacc,
-    wl, ws1s, ws1r, ws2s, ws2r, wds, wdr, a1s, a1r, a2s, a2r, a3s, a3r,
+    inp, outs, wl, ws1s, ws1r, ws2s, ws2r, wds, wdr, a1s, a1r, a2s, a2r, a3s, a3r,
     hs, hr, i1s, i1r, i2s, i2r, i3s, i3r, sts, str_, fs, fr, fds, fdr,
 ):
     row, col = lax.axis_index("row"), lax.axis_index("col")
@@ -182,15 +183,14 @@
     def eye():
         return lax.broadcasted_iota(jnp.int32, (256, 256), 0) == lax.broadcasted_iota(jnp.int32, (256, 256), 1)
 
-    def multiply(l, src, held):
-        acc[...] = held.reshape(256, 512).astype(F32)
-
-        def body(q, carry):
-            acc[...] += jnp.dot(src(q), wv[l, q].reshape(512, 512), preferred_element_type=F32)
-            return carry
-
-        lax.fori_loop(0, 8, body, 0)
-        new = acc[...].astype(BF16)
+    def multiply(l, qs, src, first):
+        total = jnp.dot(src(qs[0]), wv[l, qs[0]].reshape(512, 512), preferred_element_type=F32)
+        for q in qs[1:]:
+            total = total + jnp.dot(src(q), wv[l, q].reshape(512, 512), preferred_element_type=F32)
+        acc[...] = total if first else acc[...] + total
+
+    def finish(l, held):
+        new = (held.reshape(256, 512).astype(F32) + acc[...]).astype(BF16)
         a[l + 1, qme] = new.reshape(2, 128, 512)
         val = new.astype(F32)
         sq = val * val
@@ -282,21 +282,32 @@
 
         lax.fori_loop(k0, k1, body, 0)
 
-    for l in range(LAYERS):
-        load_own(l)
-
     barrier = pltpu.get_barrier_semaphore()
     peers = [cube_dev(fl) for fl in CUBE] + [far_dev(fl) for fl in FAR] + [partner]
     for dev in peers:
         pl.semaphore_signal(barrier, inc=1, device_id=dev, device_id_type=MESH)
-    pl.semaphore_wait(barrier, len(peers))
-
-    w1_send(0)
-
+    inputs = [
+        pltpu.make_async_copy(src, dst, inp.at[k])
+        for k, (src, dst) in enumerate(
+            ((ids_in, ids_ref), (rows_in, rows_ref), (embed_in, embed_ref), (gain_in, gain_ref))
+        )
+    ]
+    for copy in inputs:
+        copy.start()
+    for l in range(LAYERS):
+        load_own(l)
+
+    inputs[0].wait()
     ids = 8.0 - ids_ref[...].astype(F32)
     i0 = lax.broadcasted_iota(jnp.int32, (32, 32), 0)
     i1 = lax.broadcasted_iota(jnp.int32, (32, 32), 1)
     code = jnp.sum(jnp.where(i0 == i1, ids, 0.0), axis=1, keepdims=True)
+    lane = lax.broadcasted_iota(jnp.int32, (32, 128), 1)
+    sub = lax.broadcasted_iota(jnp.int32, (32, 128), 0)
+    line = jnp.sum(jnp.where(lane == sub + (col % 4) * 32, code, 0.0), axis=0, keepdims=True)
+    idg[zo, yo * 2 + x] = jnp.broadcast_to(line, (8, 128)).astype(jnp.int32)
+    for copy in inputs[1:]:
+        copy.wait()
     own_rows = pl.ds(pl.multiple_of(yo * 64 + x * 32, 32), 32)
     square = jnp.zeros((32, 128), F32)
     tiles = [
@@ -320,14 +331,11 @@
         lanes = slice(s * 128, s * 128 + 128)
         u = h0s[q, :, lanes].astype(F32) * half * gp[0, q, 0:1, lanes]
         a[0, q, zo, own_rows, lanes] = (u + u * jnp.tanh(u)).astype(BF16)
+    h0[zo, own_rows, :] = h0s[qme]
+
+    pl.semaphore_wait(barrier, len(peers))
     step1(0)
-    h0[zo, own_rows, :] = h0s[qme]
-    for k in range(7):
-        h_copy(k).start()
-    lane = lax.broadcasted_iota(jnp.int32, (32, 128), 1)
-    sub = lax.broadcasted_iota(jnp.int32, (32, 128), 0)
-    line = jnp.sum(jnp.where(lane == sub + (col % 4) * 32, code, 0.0), axis=0, keepdims=True)
-    idg[zo, yo * 2 + x] = jnp.broadcast_to(line, (8, 128)).astype(jnp.int32)
+    w1_send(0)
     for k in range(7):
         id1(k).start()
 
@@ -336,19 +344,22 @@
     w1_send(1)
     step2(0, 1)
     for k in range(7):
+        h_copy(k).start()
+    step3(0)
+    for k in range(7):
         id1(k, True).wait_recv()
     g, b = far_at(ME)
     idf[g, :, b] = idg[...]
     for k in range(7):
         id2(k).start()
-    for k in range(7):
-        h_copy(k, True).wait_recv()
-    step3(0)
     w1_rest(0)
     step3_in(0)
     w2_in(0)
     wd_in(0)
-    multiply(0, lambda q: a[0, q].reshape(256, 512), h0[...])
+    multiply(0, range(8), lambda q: a[0, q].reshape(256, 512), True)
+    for k in range(7):
+        h_copy(k, True).wait_recv()
+    finish(0, h0[...])
 
     def layer(l, carry):
         for k in range(7):
@@ -366,8 +377,9 @@
         step2(l, 0)
         activate(l, qme)
         step2(l, 1)
-        for d in range(3):
-            activate(l, cube_q(CUBE[d]))
+        near = [cube_q(CUBE[d]) for d in range(3)]
+        for q in near:
+            activate(l, q)
         w1_rest(l)
         step3(l)
 
@@ -388,13 +400,16 @@
         def _():
             selection((l - 2) * 8, (l - 1) * 8)
 
-        for d in range(3):
-            activate(l, cube_q(pair(d)))
+        mid = [cube_q(pair(d)) for d in range(3)]
+        for q in mid:
+            activate(l, q)
         w2_in(l)
+        wd_in(l)
+        multiply(l, [qme] + near + mid, lambda q: act[q], True)
         step3_in(l)
         activate(l, cube_q(ALL))
-        wd_in(l)
-        multiply(l, lambda q: act[q], a[l, qme])
+        multiply(l, [cube_q(ALL)], lambda q: act[q], False)
+        finish(l, a[l, qme])
         return carry
 
     lax.fori_loop(1, LAYERS, layer, 0)
@@ -403,19 +418,37 @@
         out1(k).start()
     f[g, :, b] = a[LAYERS, qme, :, :, cols(slot(0, 0))]
     out2(0).start()
-    for k in range(7):
+
+    def place(first, last, groups):
+        for m in range(4):
+            lines = slice(m * 256, m * 256 + 256)
+            total = None if first else oacc[lines]
+            for at in groups:
+                for k in range(2):
+                    part = jnp.dot(
+                        pm[at * 2 + k, lines], f[at, k].reshape(256, 128), preferred_element_type=F32
+                    )
+                    total = part if total is None else total + part
+            if last:
+                outv[lines] = total.astype(BF16)
+                pltpu.make_async_copy(outv.at[lines], out_ref.at[lines], outs.at[m]).start()
+            else:
+                oacc[lines] = total
+
+    for k in range(3):
         out1(k, True).wait_recv()
         out2(k + 1).start()
+    place(True, False, [(xh * 2 + core) * 2 + k for k in range(2)])
+    for k in range(3, 7):
+        out1(k, True).wait_recv()
+        out2(k + 1).start()
+    place(False, False, [((1 - xh) * 2 + core) * 2 + k for k in range(2)])
     for k in range(8):
         out2(k, True).wait_recv()
-    oacc[...] = jnp.zeros_like(oacc)
-
-    def place(k, carry):
-        oacc[...] += jnp.dot(pm[k], f[k // 2, k % 2].reshape(256, 128), preferred_element_type=F32)
-        return carry
-
-    lax.fori_loop(0, 16, place, 0)
-    out_ref[...] = oacc[...].astype(BF16)
+    place(False, True, [(k // 2 * 2 + 1 - core) * 2 + k % 2 for k in range(4)])
+    for m in range(4):
+        lines = slice(m * 256, m * 256 + 256)
+        pltpu.make_async_copy(outv.at[lines], out_ref.at[lines], outs.at[m]).wait()
 
     def drain(l, carry):
         for k in range(2):
@@ -462,9 +495,14 @@
     return pl.pallas_call(
         kernel,
         out_shape=jax.ShapeDtypeStruct((1024, 128), BF16),
-        in_specs=[pl.BlockSpec(memory_space=pltpu.VMEM)] * 4 + [pl.BlockSpec(memory_space=pl.ANY)],
-        out_specs=pl.BlockSpec(memory_space=pltpu.VMEM),
+        in_specs=[pl.BlockSpec(memory_space=pl.ANY)] * 5,
+        out_specs=pl.BlockSpec(memory_space=pl.ANY),
         scratch_shapes=[
+            vmem((32, 4096), BF16),
+            vmem((1, 32), jnp.int32),
+            vmem((8, 4096), BF16),
+            vmem((4, 4096), F32),
+            vmem((1024, 128), BF16),
             vmem((4, 8, 4, 128, 512), BF16),
             vmem((5, 8, 2, 128, 512), BF16),
             vmem((8, 256, 512), BF16),
@@ -480,6 +518,8 @@
             vmem((5, 8, 8, 256), F32),
             vmem((256, 128), F32),
             vmem((1024, 128), F32),
+            dma((4,)),
+            dma((4,)),
             dma((4,)),
             *pairs(4, 2, 2),
             *pairs(4, 2),

time: 118 us -> 106 us (0.90)
  Pallas kernels: 116 us -> 104 us
    pallas_call x1, Pallas kernels: 116 us -> 104 us  [shards(): pl.pallas_call(kernel, out_shape=jax.ShapeDtypeStruct((1024, 128), BF16),...]
where the time goes in v2:
time: 106 us
  Pallas kernels  104 us (98%)
  local copies, waits for them, and re-layouts  1.67 us (2%)
    pallas_call x1, Pallas kernels, shards(): pl.pallas_call(kernel, out_shape=jax.ShapeDtypeStruct((1024, 128), BF16),...  104 us

profile of v2, /device:TPU:1, one launch (start us, length us, event | category | flops | bytes accessed | tf_op | source)
XLA Modules:
  0.0 105.7 jit_solution(16411757643876805365)
XLA Ops:
  0.0 104.0 %shard_map.55 = bf16[1024,128]{1,0:T(8,128)(2,1)} custom-call(bf16[32,4096]{1,0:T(8,128)(2,1)} %rows_in.1, s32[1,32]{1,0:T(1,128)} %bitcast.3, bf16[8,4096]{1,0:T(8,128)(2,1)} %embed_in.1, f32[4,4096]{1,0:T(4,128)} %gain_in.1, bf16[4,4,4,2,128,128]{5,4,3,2,1,0:T(8,128)(2,1)} %bitcast.2), custom_call_target="tpu_custom_call" | custom-call | tf_op jit(solution)/shard_map/pallas_call | solution.py:495
  104.0 1.7 %copy.7 = bf16[1024,128]{1,0:T(8,128)(2,1)} copy(bf16[1024,128]{1,0:T(8,128)(2,1)} %shard_map.55) | data formatting | bytes 524288

commit v3 on v2

v3 whole, which is shorter than its diff:
```python
import functools

import jax
import jax.numpy as jnp
from jax import lax
from jax.experimental import pallas as pl
from jax.experimental.pallas import tpu as pltpu
from jax.sharding import PartitionSpec as P

MESH = pl.DeviceIdType.MESH
F32 = jnp.float32
BF16 = jnp.bfloat16
EPS = 1e-06
LAYERS = 4
CUBE = [(1, 0, 0), (0, 1, 0), (0, 0, 1), (1, 1, 0), (0, 1, 1), (1, 0, 1), (1, 1, 1)]
NEXT = (1, 2, 0)
PREV = (2, 0, 1)
THIRDS = (((0, 2), (2, 1), (3, 1)), ((4, 1), (5, 2), (7, 1)))
ROW_THIRDS = ((0, 48), (48, 48), (96, 32))
FAR = [(i // 4, (i // 2) % 2, i % 2) for i in range(1, 8)]


def flip(bit, on):
    return 1 - bit if on else bit


def kernel(
    rows_in, ids_in, embed_in, gain_in, w_ref, out_ref,
    rows_ref, ids_ref, embed_ref, gain_ref, outv,
    wv, a, act, acc, h0s, h0, gp, pm, f, idg, idf, pos, stat, invb, oacc,
    inp, outs, wl, wsend, w1r, w2r, wdr, asend, a1r, a2r, a3r, tsend, tr,
    hs, hr, i1s, i1r, i2s, i2r, i3s, i3r, fs, fr, fds, fdr,
):
    row, col = lax.axis_index("row"), lax.axis_index("col")
    xh, core = row // 2, row % 2
    z, y, x = col // 8, (col // 2) % 4, col % 2
    zh, zo, yh, yo = z // 2, z % 2, y // 2, y % 2
    zl, yl = zo + zh - 2 * zo * zh, yo + yh - 2 * yo * yh
    qme = zl * 4 + yl * 2 + x

    def cube_dev(fl):
        return (row, (zh * 2 + flip(zo, fl[2])) * 8 + (yh * 2 + flip(yo, fl[1])) * 2 + flip(x, fl[0]))

    def cube_q(fl):
        return flip(zl, fl[2]) * 4 + flip(yl, fl[1]) * 2 + flip(x, fl[0])

    def far_dev(fl):
        zz = 3 - z if fl[1] else z
        yy = 3 - y if fl[2] else y
        return (flip(xh, fl[0]) * 2 + core, zz * 8 + yy * 2 + x)

    def slot(fa, fb):
        return flip(zh, fa) * 2 + flip(yh, fb)

    def cols(s):
        return pl.ds(pl.multiple_of(s * 128, 128), 128)

    partner = (xh * 2 + (1 - core), col)
    links = [cube_dev(CUBE[d]) for d in range(3)]
    wlinks = [far_dev((0, 0, 1)), far_dev((0, 1, 0))]

    def remote(src, dst, ss, rs, dev):
        return pltpu.make_async_remote_copy(
            src_ref=src, dst_ref=dst, send_sem=ss, recv_sem=rs, device_id=dev, device_id_type=MESH
        )

    def both(ref, ss, rs, dev):
        return remote(ref, ref, ss, rs, dev)

    def arrived(ref, sem):
        both(ref, sem, sem, partner).wait_recv()

    def left(ref, sem):
        both(ref, sem, sem, partner).wait_send()

    def load_own(l):
        for zz in range(4):
            for yy in range(4):
                q0 = min(zz, 3 - zz) * 4 + min(yy, 3 - yy) * 2
                pltpu.make_async_copy(
                    w_ref.at[l, zz, yy],
                    wv.at[l, slot(0, 0), pl.ds(q0, 2), (zz // 2) * 2 + yy // 2],
                    wl.at[l],
                ).start()

    def own_loaded(l):
        whole = wv.at[l, slot(0, 0)]
        pltpu.make_async_copy(whole, whole, wl.at[l]).wait()

    def wpart(l, fa, fb, q0, n):
        return wv.at[l, slot(fa, fb), pl.ds(q0, n)]

    def w1(l, k, j):
        return both(wpart(l, 0, 0, core * 4 + 2 * j, 2), wsend.at[l], w1r.at[l, int(k != j)], wlinks[k])

    def w2(l, k):
        fa, fb = (1, 0) if k == 0 else (0, 1)
        return both(wpart(l, fa, fb, core * 4 + 2 * (1 - k), 2), wsend.at[l], w2r.at[l], wlinks[k])

    def wd(l, k):
        fa, fb = ((0, 1), (1, 0), (1, 1))[k]
        return both(wpart(l, fa, fb, core * 4, 4), wsend.at[l], wdr.at[l], partner)

    def w1_send(l):
        own_loaded(l)
        for k, j in ((0, 0), (1, 1), (0, 1), (1, 0)):
            w1(l, k, j).start()

    def w1_first(l):
        arrived(wv.at[l, 0, pl.ds(0, 4)], w1r.at[l, 0])
        w2(l, 1).start()
        w2(l, 0).start()

    def w1_rest(l):
        arrived(wv.at[l, 0, pl.ds(0, 4)], w1r.at[l, 1])
        wd(l, 0).start()
        wd(l, 1).start()

    def w2_in(l):
        arrived(wv.at[l, 0, pl.ds(0, 4)], w2r.at[l])
        wd(l, 2).start()

    def wd_in(l):
        arrived(wv.at[l, pl.ds(0, 3), pl.ds(0, 4)], wdr.at[l])

    def drain_weights(l):
        left(wv.at[l, pl.ds(0, 3)], wsend.at[l])

    def zero(l):
        return isinstance(l, int) and l == 0

    def chunk(l, fl, i):
        if zero(l):
            at = pl.ds(pl.multiple_of(flip(yo, fl[1]) * 64 + flip(x, fl[0]) * 32, 32), 32)
            return a.at[0, pl.ds(4 * i, 4), flip(zo, fl[2]), at, :]
        return a.at[l, cube_q(fl), i]

    def third(l, fl, e, i):
        if zero(l):
            at = pl.ds(pl.multiple_of(flip(yo, fl[1]) * 64 + flip(x, fl[0]) * 32, 32), 32)
            return a.at[0, pl.ds(*THIRDS[i][e]), flip(zo, fl[2]), at, :]
        return a.at[l, cube_q(fl), i, pl.ds(*ROW_THIRDS[e]), :]

    ME, ALL = (0, 0, 0), (1, 1, 1)

    def pair(d):
        e = PREV[d]
        return tuple(int(k in (d, e)) for k in range(3))

    def s1(l, d, i):
        return both(chunk(l, ME, i), asend.at[l], a1r.at[l, i], links[d])

    def s2(l, d, i):
        return both(chunk(l, CUBE[PREV[d]], i), asend.at[l], a2r.at[l, i], links[d])

    def s3(l, d, i):
        return both(third(l, pair(PREV[d]), d, i), asend.at[l], a3r.at[l, i], links[d])

    def step1(l, i):
        for d in range(3):
            s1(l, d, i).start()

    def step2(l, i):
        arrived(a.at[l, pl.ds(0, 3), 0], a1r.at[l, i])
        for d in range(3):
            s2(l, d, i).start()

    def step3(l, i):
        arrived(a.at[l, pl.ds(0, 3), 0], a2r.at[l, i])
        for d in range(3):
            s3(l, d, i).start()

    def step3_in(l, i):
        arrived(a.at[l, 0, 0], a3r.at[l, i])

    def drain_act(l):
        left(a.at[l, pl.ds(0, 7)], asend.at[l])

    def stat_copy(l, k, i):
        return both(stat.at[l, i, qme], tsend.at[l], tr.at[l, i], cube_dev(CUBE[k]))

    def drain_stats(l):
        left(stat.at[l, :, pl.ds(0, 7)], tsend.at[l])

    def eye():
        return lax.broadcasted_iota(jnp.int32, (128, 128), 0) == lax.broadcasted_iota(jnp.int32, (128, 128), 1)

    def weight(l, q):
        return jnp.concatenate([wv[l, k, q].reshape(512, 128) for k in range(4)], axis=1)

    def multiply(l, i, qs, src, first):
        total = jnp.dot(src(qs[0]), weight(l, qs[0]), preferred_element_type=F32)
        for q in qs[1:]:
            total = total + jnp.dot(src(q), weight(l, q), preferred_element_type=F32)
        acc[i] = total if first else acc[i] + total

    def finish(l, i, held):
        new = (held.astype(F32) + acc[i]).astype(BF16)
        a[l + 1, qme, i] = new
        val = new.astype(F32)
        sq = val * val
        sq = (sq[:, 0:128] + sq[:, 128:256]) + (sq[:, 256:384] + sq[:, 384:512])
        total = jnp.sum(sq, axis=1, keepdims=True)
        line = jnp.sum(jnp.where(eye(), total, 0.0), axis=0, keepdims=True)
        stat[l + 1, i, qme] = jnp.broadcast_to(line, (8, 128))

    def begin(l, i):
        for k in range(7):
            stat_copy(l, k, i).start()
        step1(l, i)

    def read_stats(l, i):
        arrived(stat.at[l, i, pl.ds(0, 7)], tr.at[l, i])
        total = stat[l, i, 0]
        for q in range(1, 8):
            total = total + stat[l, i, q]
        half = 0.5 * lax.rsqrt(total[0:1] * (1.0 / 4096.0) + EPS)
        tall = jnp.sum(jnp.where(eye(), half, 0.0), axis=1, keepdims=True)
        invb[i] = jnp.broadcast_to(tall, (128, 128))

    def activate(l, i, q):
        for t in range(4):
            c = slice(t * 128, t * 128 + 128)
            u = a[l, q, i, :, c].astype(F32) * invb[i] * gp[l, q, 0:1, c]
            act[q, i, :, c] = (u + u * jnp.tanh(u)).astype(BF16)

    def h_copy(k):
        dst = h0.at[zo, pl.ds(pl.multiple_of(yo * 64 + x * 32, 32), 32), :]
        return remote(h0s.at[cube_q(CUBE[k])], dst, hs, hr, cube_dev(CUBE[k]))

    def id1(k):
        return both(idg.at[zo, yo * 2 + x], i1s, i1r, cube_dev(CUBE[k]))

    def far_at(fl):
        return (flip(xh, fl[0]) * 2 + core) * 2 + flip(zh, fl[1]), flip(yh, fl[2])

    g_me, b_me = far_at(ME)
    seven = stat.at[0, 0, pl.ds(0, 7)]

    def id2(k):
        return remote(idg, idf.at[g_me, :, b_me], i2s, i2r, far_dev(FAR[k]))

    def id3(k):
        return both(idf.at[pl.ds((k * 2 + core) * 2, 2)], i3s, i3r, partner)

    def out1(k, i):
        src = a.at[LAYERS, qme, i, :, cols(slot(FAR[k][1], FAR[k][2]))]
        return remote(src, f.at[g_me, i, b_me], fs, fr.at[k], far_dev(FAR[k]))

    def out_begin(i):
        for k in range(7):
            out1(k, i).start()
        f[g_me, i, b_me] = a[LAYERS, qme, i, :, cols(slot(0, 0))]

    def out2(k):
        fl = ([ME] + FAR)[k]
        g, b = far_at(fl)
        return both(f.at[g, :, b], fds, fdr, partner)

    def positions():
        spread = idf[...].reshape(1024, 128).astype(F32).astype(BF16)
        k = lax.broadcasted_iota(jnp.int32, (32, 1024), 0)
        j = lax.broadcasted_iota(jnp.int32, (32, 1024), 1)
        pick = jnp.where((j // 32 == k) & (j % 8 == 0), 1.0, 0.0).astype(BF16)
        code = jnp.dot(pick, spread, preferred_element_type=F32)
        member = jnp.concatenate([jnp.where(code == 8.0 - t, 1.0, 0.0) for t in range(8)], axis=0).astype(BF16)
        i0 = lax.broadcasted_iota(jnp.int32, (128, 128), 0)
        i1 = lax.broadcasted_iota(jnp.int32, (128, 128), 1)
        upper = jnp.where(i0 < i1, 1.0, 0.0).astype(BF16)
        within = jnp.dot(member, upper, preferred_element_type=F32)
        count = jnp.dot(member, jnp.ones((128, 128), BF16), preferred_element_type=F32).astype(BF16)
        j0 = lax.broadcasted_iota(jnp.int32, (256, 256), 0)
        j1 = lax.broadcasted_iota(jnp.int32, (256, 256), 1)
        lower = jnp.where(j1 < j0, 1.0, 0.0).astype(BF16)
        place = jnp.dot(lower, count, preferred_element_type=F32) + within
        where = jnp.full((32, 128), -1.0, F32)
        for t in range(8):
            where = jnp.where(code == 8.0 - t, place[t * 32 : t * 32 + 32], where)
        for k in range(32):
            pos[k, 0:1, :] = where[k : k + 1]

    def selection(k0, k1):
        slots = (lax.broadcasted_iota(jnp.int32, (1024, 128), 0) * 4 + row).astype(F32)

        def body(k, carry):
            for half in range(2):
                hit = slots == pos[k * 2 + half, 0:1, :]
                pm[k, :, half * 128 : half * 128 + 128] = jnp.where(hit, 1.0, 0.0).astype(BF16)
            return carry

        lax.fori_loop(k0, k1, body, 0)

    barrier = pltpu.get_barrier_semaphore()
    peers = [cube_dev(fl) for fl in CUBE] + [far_dev(fl) for fl in FAR] + [partner]
    for dev in peers:
        pl.semaphore_signal(barrier, inc=1, device_id=dev, device_id_type=MESH)
    inputs = [
        pltpu.make_async_copy(src, dst, inp.at[k])
        for k, (src, dst) in enumerate(
            ((ids_in, ids_ref), (rows_in, rows_ref), (embed_in, embed_ref), (gain_in, gain_ref))
        )
    ]
    for copy in inputs:
        copy.start()
    for l in range(LAYERS):
        load_own(l)

    inputs[0].wait()
    ids = 8.0 - ids_ref[...].astype(F32)
    i0 = lax.broadcasted_iota(jnp.int32, (32, 32), 0)
    i1 = lax.broadcasted_iota(jnp.int32, (32, 32), 1)
    code = jnp.sum(jnp.where(i0 == i1, ids, 0.0), axis=1, keepdims=True)
    lane = lax.broadcasted_iota(jnp.int32, (32, 128), 1)
    sub = lax.broadcasted_iota(jnp.int32, (32, 128), 0)
    line = jnp.sum(jnp.where(lane == sub + (col % 4) * 32, code, 0.0), axis=0, keepdims=True)
    idg[zo, yo * 2 + x] = jnp.broadcast_to(line, (8, 128)).astype(jnp.int32)
    for copy in inputs[1:]:
        copy.wait()
    own_rows = pl.ds(pl.multiple_of(yo * 64 + x * 32, 32), 32)
    square = jnp.zeros((32, 128), F32)
    tiles = [
        (q, s, ((q // 4 if s < 2 else 3 - q // 4) * 8 + ((q // 2) % 2 if s % 2 == 0 else 3 - (q // 2) % 2) * 2 + q % 2) * 128)
        for q in range(8)
        for s in range(4)
    ]
    for q, s, c in tiles:
        table = embed_ref[:, c : c + 128].astype(F32)
        term = jnp.zeros((32, 128), F32)
        for t in range(8):
            term = jnp.where(code == 8.0 - t, table[t : t + 1], term)
        start = (rows_ref[:, c : c + 128].astype(F32) + term).astype(BF16)
        h0s[q, :, s * 128 : s * 128 + 128] = start
        start = start.astype(F32)
        square = square + start * start
        for l in range(LAYERS):
            gp[l, q, 0:1, s * 128 : s * 128 + 128] = gain_ref[l : l + 1, c : c + 128]
    half = 0.5 * lax.rsqrt(jnp.sum(square, axis=1, keepdims=True) * (1.0 / 4096.0) + EPS)
    for q, s, c in tiles:
        lanes = slice(s * 128, s * 128 + 128)
        u = h0s[q, :, lanes].astype(F32) * half * gp[0, q, 0:1, lanes]
        a[0, q, zo, own_rows, lanes] = (u + u * jnp.tanh(u)).astype(BF16)
    h0[zo, own_rows, :] = h0s[qme]

    pl.semaphore_wait(barrier, len(peers))
    for k in range(7):
        id1(k).start()
    step1(0, 0)
    step1(0, 1)
    w1_send(0)

    step2(0, 0)
    w1_first(0)
    w1_send(1)
    step2(0, 1)
    step3(0, 0)
    for k in range(7):
        h_copy(k).start()
    step3(0, 1)
    arrived(seven, i1r)
    idf[g_me, :, b_me] = idg[...]
    for k in range(7):
        id2(k).start()
    w1_rest(0)
    step3_in(0, 0)
    step3_in(0, 1)
    w2_in(0)
    wd_in(0)
    multiply(0, 0, range(8), lambda q: a[0, q, 0], True)
    arrived(h0s.at[pl.ds(0, 7)], hr)
    finish(0, 0, h0[0])
    begin(1, 0)
    multiply(0, 1, range(8), lambda q: a[0, q, 1], True)
    finish(0, 1, h0[1])
    begin(1, 1)

    def layer(l, carry):
        near = [cube_q(CUBE[d]) for d in range(3)]
        mid = [cube_q(pair(d)) for d in range(3)]
        w1_first(l)

        @pl.when(l < LAYERS - 1)
        def _():
            w1_send(l + 1)

        read_stats(l, 0)
        activate(l, 0, qme)
        step2(l, 0)
        read_stats(l, 1)
        activate(l, 1, qme)
        step2(l, 1)
        for q in near:
            activate(l, 0, q)
        step3(l, 0)
        for q in near:
            activate(l, 1, q)
        w1_rest(l)
        step3(l, 1)

        @pl.when(l == 1)
        def _():
            arrived(idf.at[pl.ds(0, 7), :, 0], i2r)
            for k in range(2):
                id3(k).start()
            drain_act(0)
            left(h0s.at[pl.ds(0, 7)], hs)
            left(seven, i1s)

        @pl.when(l == 2)
        def _():
            arrived(idf.at[pl.ds(0, 4)], i3r)
            positions()
            left(idf.at[pl.ds(0, 7), :, 0], i2s)

        @pl.when(l >= 2)
        def _():
            selection((l - 2) * 8, (l - 1) * 8)
            drain_act(l - 1)
            drain_stats(l - 1)

        drain_weights(l - 1)
        for q in mid:
            activate(l, 0, q)
        w2_in(l)
        for q in mid:
            activate(l, 1, q)
        wd_in(l)
        for i in range(2):
            multiply(l, i, [qme] + near + mid, lambda q: act[q, i], True)
            step3_in(l, i)
            activate(l, i, cube_q(ALL))
            multiply(l, i, [cube_q(ALL)], lambda q: act[q, i], False)
            finish(l, i, a[l, qme, i])

            @pl.when(l < LAYERS - 1)
            def _():
                begin(l + 1, i)

            @pl.when(l == LAYERS - 1)
            def _():
                out_begin(i)

        return carry

    lax.fori_loop(1, LAYERS, layer, 0)

    out2(0).start()
    drain_weights(LAYERS - 1)
    drain_act(LAYERS - 1)
    drain_stats(LAYERS - 1)
    left(idf.at[pl.ds(0, 4)], i3s)

    def place(first, last, groups):
        for m in range(4):
            lines = slice(m * 256, m * 256 + 256)
            total = None if first else oacc[lines]
            for at in groups:
                for k in range(2):
                    part = jnp.dot(
                        pm[at * 2 + k, lines], f[at, k].reshape(256, 128), preferred_element_type=F32
                    )
                    total = part if total is None else total + part
            if last:
                outv[lines] = total.astype(BF16)
                pltpu.make_async_copy(outv.at[lines], out_ref.at[lines], outs).start()
            else:
                oacc[lines] = total

    for k in range(3):
        arrived(f.at[0, :, 0], fr.at[k])
        out2(k + 1).start()
    place(True, False, [(xh * 2 + core) * 2 + k for k in range(2)])
    for k in range(3, 7):
        arrived(f.at[0, :, 0], fr.at[k])
        out2(k + 1).start()
    place(False, False, [((1 - xh) * 2 + core) * 2 + k for k in range(2)])
    arrived(f.at[pl.ds(0, 4)], fdr)
    place(False, True, [(k // 2 * 2 + 1 - core) * 2 + k % 2 for k in range(4)])
    pltpu.make_async_copy(outv, out_ref, outs).wait()

    left(f.at[pl.ds(0, 7), :, 0], fs)
    left(f.at[pl.ds(0, 4)], fds)


def shards(rows, task_ids, task_embed, norm_gain, layer_weight):
    dma = pltpu.SemaphoreType.DMA
    vmem = pltpu.VMEM
    return pl.pallas_call(
        kernel,
        out_shape=jax.ShapeDtypeStruct((1024, 128), BF16),
        in_specs=[pl.BlockSpec(memory_space=pl.ANY)] * 5,
        out_specs=pl.BlockSpec(memory_space=pl.ANY),
        scratch_shapes=[
            vmem((32, 4096), BF16),
            vmem((1, 32), jnp.int32),
            vmem((8, 4096), BF16),
            vmem((4, 4096), F32),
            vmem((1024, 128), BF16),
            vmem((4, 4, 8, 4, 128, 128), BF16),
            vmem((5, 8, 2, 128, 512), BF16),
            vmem((8, 2, 128, 512), BF16),
            vmem((2, 128, 512), F32),
            vmem((8, 32, 512), BF16),
            vmem((2, 128, 512), BF16),
            vmem((4, 8, 8, 512), F32),
            vmem((16, 1024, 256), BF16),
            vmem((8, 2, 2, 128, 128), BF16),
            vmem((2, 4, 8, 128), jnp.int32),
            vmem((8, 2, 2, 4, 8, 128), jnp.int32),
            vmem((32, 8, 128), F32),
            vmem((5, 2, 8, 8, 128), F32),
            vmem((2, 128, 128), F32),
            vmem((1024, 128), F32),
            dma((4,)),
            dma,
            dma((4,)),
            dma((4,)),
            dma((4, 2)),
            dma((4,)),
            dma((4,)),
            dma((4,)),
            dma((4, 2)),
            dma((4, 2)),
            dma((4, 2)),
            dma((4,)),
            dma((4, 2)),
            *[dma] * 8,
            dma,
            dma((7,)),
            dma,
            dma,
        ],
        compiler_params=pltpu.CompilerParams(
            collective_id=0, has_side_effects=True, vmem_limit_bytes=60 * 1024 * 1024
        ),
    )(
        rows,
        task_ids.reshape(1, 32),
        task_embed,
        norm_gain,
        layer_weight.reshape(4, 4, 4, 2, 128, 128),
    )


def solution(mesh):
    return jax.shard_map(
        shards,
        mesh=mesh,
        in_specs=(P(("row", "col"), None), P(("row", "col")), P(), P(), P(None, None, "col")),
        out_specs=P("row", "col"),
        check_vma=False,
    )
```

time: 106 us -> 101 us (0.953)
  Pallas kernels: 104 us -> 99.4 us
    pallas_call x1, Pallas kernels: 104 us -> 99.4 us  [shards(): pl.pallas_call(kernel, out_shape=jax.ShapeDtypeStruct((1024, 128), BF16),...]
where the time goes in v3:
time: 101 us
  Pallas kernels  99.4 us (98%)
  local copies, waits for them, and re-layouts  1.67 us (2%)
    pallas_call x1, Pallas kernels, shards(): pl.pallas_call(kernel, out_shape=jax.ShapeDtypeStruct((1024, 128), BF16),...  99.4 us

profile of v3, /device:TPU:1, one launch (start us, length us, event | category | flops | bytes accessed | tf_op | source)
XLA Modules:
  0.0 101.1 jit_solution(8653817371850887023)
XLA Ops:
  0.0 99.4 %shard_map.55 = bf16[1024,128]{1,0:T(8,128)(2,1)} custom-call(bf16[32,4096]{1,0:T(8,128)(2,1)} %rows_in.1, s32[1,32]{1,0:T(1,128)} %bitcast.3, bf16[8,4096]{1,0:T(8,128)(2,1)} %embed_in.1, f32[4,4096]{1,0:T(4,128)} %gain_in.1, bf16[4,4,4,2,128,128]{5,4,3,2,1,0:T(8,128)(2,1)} %bitcast.2), custom_call_target="tpu_custom_call" | custom-call | tf_op jit(solution)/shard_map/pallas_call | solution.py:487
  99.4 1.7 %copy.7 = bf16[1024,128]{1,0:T(8,128)(2,1)} copy(bf16[1024,128]{1,0:T(8,128)(2,1)} %shard_map.55) | data formatting | bytes 524288

commit v4 on v3

--- a/solution.py
+++ b/solution.py
@@ -26,10 +26,10 @@
 
 def kernel(
     rows_in, ids_in, embed_in, gain_in, w_ref, out_ref,
-    rows_ref, ids_ref, embed_ref, gain_ref, outv,
-    wv, a, act, acc, h0s, h0, gp, pm, f, idg, idf, pos, stat, invb, oacc,
-    inp, outs, wl, wsend, w1r, w2r, wdr, asend, a1r, a2r, a3r, tsend, tr,
-    hs, hr, i1s, i1r, i2s, i2r, i3s, i3r, fs, fr, fds, fdr,
+    rows_ref, ids_ref, embed_ref, gain_ref,
+    wv, a, act, acc, gp, pm, f, idg, idf, pos, stat, invb, oacc,
+    inp, wl, wsend, w1r, w2r, wdr, asend, a1r, a2r, a3r, tsend, tr,
+    i1s, i1r, i2s, i2r, i3s, i3r, fs, fr, fds, fdr,
 ):
     row, col = lax.axis_index("row"), lax.axis_index("col")
     xh, core = row // 2, row % 2
@@ -177,10 +177,10 @@
         left(a.at[l, pl.ds(0, 7)], asend.at[l])
 
     def stat_copy(l, k, i):
-        return both(stat.at[l, i, qme], tsend.at[l], tr.at[l, i], cube_dev(CUBE[k]))
+        return both(stat.at[l, i, qme, pl.ds(0, 1)], tsend.at[l], tr.at[l, i], cube_dev(CUBE[k]))
 
     def drain_stats(l):
-        left(stat.at[l, :, pl.ds(0, 7)], tsend.at[l])
+        left(stat.at[l, :, pl.ds(0, 7), pl.ds(0, 1)], tsend.at[l])
 
     def eye():
         return lax.broadcasted_iota(jnp.int32, (128, 128), 0) == lax.broadcasted_iota(jnp.int32, (128, 128), 1)
@@ -202,7 +202,7 @@
         sq = (sq[:, 0:128] + sq[:, 128:256]) + (sq[:, 256:384] + sq[:, 384:512])
         total = jnp.sum(sq, axis=1, keepdims=True)
         line = jnp.sum(jnp.where(eye(), total, 0.0), axis=0, keepdims=True)
-        stat[l + 1, i, qme] = jnp.broadcast_to(line, (8, 128))
+        stat[l + 1, i, qme, 0:1] = line
 
     def begin(l, i):
         for k in range(7):
@@ -210,11 +210,11 @@
         step1(l, i)
 
     def read_stats(l, i):
-        arrived(stat.at[l, i, pl.ds(0, 7)], tr.at[l, i])
-        total = stat[l, i, 0]
+        arrived(stat.at[l, i, pl.ds(0, 7), pl.ds(0, 1)], tr.at[l, i])
+        total = stat[l, i, 0, 0:1]
         for q in range(1, 8):
-            total = total + stat[l, i, q]
-        half = 0.5 * lax.rsqrt(total[0:1] * (1.0 / 4096.0) + EPS)
+            total = total + stat[l, i, q, 0:1]
+        half = 0.5 * lax.rsqrt(total * (1.0 / 4096.0) + EPS)
         tall = jnp.sum(jnp.where(eye(), half, 0.0), axis=1, keepdims=True)
         invb[i] = jnp.broadcast_to(tall, (128, 128))
 
@@ -224,21 +224,17 @@
             u = a[l, q, i, :, c].astype(F32) * invb[i] * gp[l, q, 0:1, c]
             act[q, i, :, c] = (u + u * jnp.tanh(u)).astype(BF16)
 
-    def h_copy(k):
-        dst = h0.at[zo, pl.ds(pl.multiple_of(yo * 64 + x * 32, 32), 32), :]
-        return remote(h0s.at[cube_q(CUBE[k])], dst, hs, hr, cube_dev(CUBE[k]))
-
     def id1(k):
-        return both(idg.at[zo, yo * 2 + x], i1s, i1r, cube_dev(CUBE[k]))
+        return both(idg.at[zo, yo * 2 + x, pl.ds(0, 1)], i1s, i1r, cube_dev(CUBE[k]))
 
     def far_at(fl):
         return (flip(xh, fl[0]) * 2 + core) * 2 + flip(zh, fl[1]), flip(yh, fl[2])
 
     g_me, b_me = far_at(ME)
-    seven = stat.at[0, 0, pl.ds(0, 7)]
+    seven = stat.at[0, 0, pl.ds(0, 7), pl.ds(0, 1)]
 
     def id2(k):
-        return remote(idg, idf.at[g_me, :, b_me], i2s, i2r, far_dev(FAR[k]))
+        return both(idf.at[g_me, :, b_me], i2s, i2r, far_dev(FAR[k]))
 
     def id3(k):
         return both(idf.at[pl.ds((k * 2 + core) * 2, 2)], i3s, i3r, partner)
@@ -258,10 +254,10 @@
         return both(f.at[g, :, b], fds, fdr, partner)
 
     def positions():
-        spread = idf[...].reshape(1024, 128).astype(F32).astype(BF16)
-        k = lax.broadcasted_iota(jnp.int32, (32, 1024), 0)
-        j = lax.broadcasted_iota(jnp.int32, (32, 1024), 1)
-        pick = jnp.where((j // 32 == k) & (j % 8 == 0), 1.0, 0.0).astype(BF16)
+        spread = idf[...].reshape(256, 128).astype(F32).astype(BF16)
+        k = lax.broadcasted_iota(jnp.int32, (32, 256), 0)
+        j = lax.broadcasted_iota(jnp.int32, (32, 256), 1)
+        pick = jnp.where(j == k * 8, 1.0, 0.0).astype(BF16)
         code = jnp.dot(pick, spread, preferred_element_type=F32)
         member = jnp.concatenate([jnp.where(code == 8.0 - t, 1.0, 0.0) for t in range(8)], axis=0).astype(BF16)
         i0 = lax.broadcasted_iota(jnp.int32, (128, 128), 0)
@@ -302,7 +298,12 @@
     ]
     for copy in inputs:
         copy.start()
-    for l in range(LAYERS):
+    load_own(0)
+    for k in range(2):
+        idf[g_me, k, b_me] = jnp.zeros((8, 128), jnp.int32)
+    pl.semaphore_wait(barrier, len(peers))
+    w1_send(0)
+    for l in range(1, LAYERS):
         load_own(l)
 
     inputs[0].wait()
@@ -313,65 +314,68 @@
     lane = lax.broadcasted_iota(jnp.int32, (32, 128), 1)
     sub = lax.broadcasted_iota(jnp.int32, (32, 128), 0)
     line = jnp.sum(jnp.where(lane == sub + (col % 4) * 32, code, 0.0), axis=0, keepdims=True)
-    idg[zo, yo * 2 + x] = jnp.broadcast_to(line, (8, 128)).astype(jnp.int32)
+    idg[zo, yo * 2 + x, 0:1] = line.astype(jnp.int32)
     for copy in inputs[1:]:
         copy.wait()
     own_rows = pl.ds(pl.multiple_of(yo * 64 + x * 32, 32), 32)
     square = jnp.zeros((32, 128), F32)
-    tiles = [
-        (q, s, ((q // 4 if s < 2 else 3 - q // 4) * 8 + ((q // 2) % 2 if s % 2 == 0 else 3 - (q // 2) % 2) * 2 + q % 2) * 128)
-        for q in range(8)
-        for s in range(4)
-    ]
-    for q, s, c in tiles:
-        table = embed_ref[:, c : c + 128].astype(F32)
-        term = jnp.zeros((32, 128), F32)
-        for t in range(8):
-            term = jnp.where(code == 8.0 - t, table[t : t + 1], term)
-        start = (rows_ref[:, c : c + 128].astype(F32) + term).astype(BF16)
-        h0s[q, :, s * 128 : s * 128 + 128] = start
-        start = start.astype(F32)
-        square = square + start * start
-        for l in range(LAYERS):
-            gp[l, q, 0:1, s * 128 : s * 128 + 128] = gain_ref[l : l + 1, c : c + 128]
-    half = 0.5 * lax.rsqrt(jnp.sum(square, axis=1, keepdims=True) * (1.0 / 4096.0) + EPS)
-    for q, s, c in tiles:
-        lanes = slice(s * 128, s * 128 + 128)
-        u = h0s[q, :, lanes].astype(F32) * half * gp[0, q, 0:1, lanes]
-        a[0, q, zo, own_rows, lanes] = (u + u * jnp.tanh(u)).astype(BF16)
-    h0[zo, own_rows, :] = h0s[qme]
-
-    pl.semaphore_wait(barrier, len(peers))
+    for q in range(8):
+        for k in range(4):
+            zz = q // 4 if k < 2 else 3 - q // 4
+            yy = (q // 2) % 2 if k % 2 == 0 else 3 - (q // 2) % 2
+            c = (zz * 8 + yy * 2 + q % 2) * 128
+            lanes = slice(k * 128, k * 128 + 128)
+            table = embed_ref[:, c : c + 128].astype(F32)
+            term = jnp.zeros((32, 128), F32)
+            for t in range(8):
+                term = jnp.where(code == 8.0 - t, table[t : t + 1], term)
+            start = (rows_ref[:, c : c + 128].astype(F32) + term).astype(BF16)
+            a[0, q, zo, own_rows, lanes] = start
+            start = start.astype(F32)
+            square = square + start * start
+            for l in range(LAYERS):
+                gp[l, q, 0:1, lanes] = gain_ref[l : l + 1, c : c + 128]
+    step1(0, 0)
+    step1(0, 1)
+    total = jnp.sum(square, axis=1, keepdims=True)
+    line = jnp.sum(jnp.where(lane == sub + yo * 64 + x * 32, total, 0.0), axis=0, keepdims=True)
+    stat[0, zo, qme, 0:1] = line
+    stat[0, 1 - zo, qme, 0:1] = jnp.zeros((1, 128), F32)
     for k in range(7):
         id1(k).start()
-    step1(0, 0)
-    step1(0, 1)
-    w1_send(0)
+        stat_copy(0, k, 0).start()
+        stat_copy(0, k, 1).start()
 
     step2(0, 0)
     w1_first(0)
     w1_send(1)
     step2(0, 1)
     step3(0, 0)
-    for k in range(7):
-        h_copy(k).start()
-    step3(0, 1)
     arrived(seven, i1r)
-    idf[g_me, :, b_me] = idg[...]
+    for k in range(2):
+        idf[g_me, k, b_me, 0:1] = idg[k, 0, 0:1] + idg[k, 1, 0:1] + idg[k, 2, 0:1] + idg[k, 3, 0:1]
     for k in range(7):
         id2(k).start()
+    read_stats(0, 0)
+    read_stats(0, 1)
+    step3(0, 1)
     w1_rest(0)
+
+    def activate_both(q, carry):
+        activate(0, 0, q)
+        activate(0, 1, q)
+        return carry
+
     step3_in(0, 0)
+    lax.fori_loop(0, 4, activate_both, 0)
+    w2_in(0)
     step3_in(0, 1)
-    w2_in(0)
+    lax.fori_loop(4, 8, activate_both, 0)
     wd_in(0)
-    multiply(0, 0, range(8), lambda q: a[0, q, 0], True)
-    arrived(h0s.at[pl.ds(0, 7)], hr)
-    finish(0, 0, h0[0])
-    begin(1, 0)
-    multiply(0, 1, range(8), lambda q: a[0, q, 1], True)
-    finish(0, 1, h0[1])
-    begin(1, 1)
+    for i in range(2):
+        multiply(0, i, range(8), lambda q: act[q, i], True)
+        finish(0, i, a[0, qme, i])
+        begin(1, i)
 
     def layer(l, carry):
         near = [cube_q(CUBE[d]) for d in range(3)]
@@ -402,7 +406,7 @@
             for k in range(2):
                 id3(k).start()
             drain_act(0)
-            left(h0s.at[pl.ds(0, 7)], hs)
+            drain_stats(0)
             left(seven, i1s)
 
         @pl.when(l == 2)
@@ -460,8 +464,7 @@
                     )
                     total = part if total is None else total + part
             if last:
-                outv[lines] = total.astype(BF16)
-                pltpu.make_async_copy(outv.at[lines], out_ref.at[lines], outs).start()
+                out_ref[lines] = total.astype(BF16)
             else:
                 oacc[lines] = total
 
@@ -475,7 +478,6 @@
     place(False, False, [((1 - xh) * 2 + core) * 2 + k for k in range(2)])
     arrived(f.at[pl.ds(0, 4)], fdr)
     place(False, True, [(k // 2 * 2 + 1 - core) * 2 + k % 2 for k in range(4)])
-    pltpu.make_async_copy(outv, out_ref, outs).wait()
 
     left(f.at[pl.ds(0, 7), :, 0], fs)
     left(f.at[pl.ds(0, 4)], fds)
@@ -486,32 +488,28 @@
     vmem = pltpu.VMEM
     return pl.pallas_call(
         kernel,
-        out_shape=jax.ShapeDtypeStruct((1024, 128), BF16),
+        out_shape=pltpu.VMEM((1024, 128), BF16),
         in_specs=[pl.BlockSpec(memory_space=pl.ANY)] * 5,
-        out_specs=pl.BlockSpec(memory_space=pl.ANY),
+        out_specs=pl.BlockSpec(memory_space=pltpu.VMEM),
         scratch_shapes=[
             vmem((32, 4096), BF16),
             vmem((1, 32), jnp.int32),
             vmem((8, 4096), BF16),
             vmem((4, 4096), F32),
-            vmem((1024, 128), BF16),
             vmem((4, 4, 8, 4, 128, 128), BF16),
             vmem((5, 8, 2, 128, 512), BF16),
             vmem((8, 2, 128, 512), BF16),
             vmem((2, 128, 512), F32),
-            vmem((8, 32, 512), BF16),
-            vmem((2, 128, 512), BF16),
             vmem((4, 8, 8, 512), F32),
             vmem((16, 1024, 256), BF16),
             vmem((8, 2, 2, 128, 128), BF16),
             vmem((2, 4, 8, 128), jnp.int32),
-            vmem((8, 2, 2, 4, 8, 128), jnp.int32),
+            vmem((8, 2, 2, 8, 128), jnp.int32),
             vmem((32, 8, 128), F32),
             vmem((5, 2, 8, 8, 128), F32),
             vmem((2, 128, 128), F32),
             vmem((1024, 128), F32),
             dma((4,)),
-            dma,
             dma((4,)),
             dma((4,)),
             dma((4, 2)),
@@ -523,7 +521,7 @@
             dma((4, 2)),
             dma((4,)),
             dma((4, 2)),
-            *[dma] * 8,
+            *[dma] * 6,
             dma,
             dma((7,)),
             dma,

time: 101 us -> 96.8 us (0.958)
  Pallas kernels: 99.4 us -> 96 us
    pallas_call x1, Pallas kernels: 99.4 us -> 96 us  [shards(): pl.pallas_call(kernel, out_shape=pltpu.VMEM((1024, 128), BF16), in_specs=...]
where the time goes in v4:
time: 96.8 us; the launch traced here: 96.7 us
  Pallas kernels  96 us (99%)
    pallas_call x1, Pallas kernels, shards(): pl.pallas_call(kernel, out_shape=pltpu.VMEM((1024, 128), BF16), in_specs=...  96 us

profile of v4, /device:TPU:1, one launch (start us, length us, event | category | flops | bytes accessed | tf_op | source)
XLA Modules:
  0.0 96.7 jit_solution(9384891364946719421)
XLA Ops:
  0.0 96.0 %shard_map.55 = bf16[1024,128]{1,0:T(8,128)(2,1)S(1)} custom-call(bf16[32,4096]{1,0:T(8,128)(2,1)} %rows_in.1, s32[1,32]{1,0:T(1,128)} %bitcast.3, bf16[8,4096]{1,0:T(8,128)(2,1)} %embed_in.1, f32[4,4096]{1,0:T(4,128)} %gain_in.1, bf16[4,4,4,2,128,128]{5,4,3,2,1,0:T(8,128)(2,1)} %bitcast.2), custom_call_target="tpu_custom_call" | custom-call | tf_op jit(solution)/shard_map/pallas_call | solution.py:489
  96.0 0.7 copy.7

commit v5 on v4

--- a/solution.py
+++ b/solution.py
@@ -188,10 +188,10 @@
     def weight(l, q):
         return jnp.concatenate([wv[l, k, q].reshape(512, 128) for k in range(4)], axis=1)
 
-    def multiply(l, i, qs, src, first):
-        total = jnp.dot(src(qs[0]), weight(l, qs[0]), preferred_element_type=F32)
+    def multiply(l, i, qs, first):
+        total = jnp.dot(act[qs[0], i], weight(l, qs[0]), preferred_element_type=F32)
         for q in qs[1:]:
-            total = total + jnp.dot(src(q), weight(l, q), preferred_element_type=F32)
+            total = total + jnp.dot(act[q, i], weight(l, q), preferred_element_type=F32)
         acc[i] = total if first else acc[i] + total
 
     def finish(l, i, held):
@@ -251,7 +251,7 @@
     def out2(k):
         fl = ([ME] + FAR)[k]
         g, b = far_at(fl)
-        return both(f.at[g, :, b], fds, fdr, partner)
+        return both(f.at[g, :, b], fds, fdr.at[k // 4], partner)
 
     def positions():
         spread = idf[...].reshape(256, 128).astype(F32).astype(BF16)
@@ -335,6 +335,8 @@
             square = square + start * start
             for l in range(LAYERS):
                 gp[l, q, 0:1, lanes] = gain_ref[l : l + 1, c : c + 128]
+    for k in range(7):
+        id1(k).start()
     step1(0, 0)
     step1(0, 1)
     total = jnp.sum(square, axis=1, keepdims=True)
@@ -342,20 +344,19 @@
     stat[0, zo, qme, 0:1] = line
     stat[0, 1 - zo, qme, 0:1] = jnp.zeros((1, 128), F32)
     for k in range(7):
-        id1(k).start()
         stat_copy(0, k, 0).start()
         stat_copy(0, k, 1).start()
 
     step2(0, 0)
-    w1_first(0)
-    w1_send(1)
-    step2(0, 1)
-    step3(0, 0)
     arrived(seven, i1r)
     for k in range(2):
         idf[g_me, k, b_me, 0:1] = idg[k, 0, 0:1] + idg[k, 1, 0:1] + idg[k, 2, 0:1] + idg[k, 3, 0:1]
     for k in range(7):
         id2(k).start()
+    w1_first(0)
+    w1_send(1)
+    step2(0, 1)
+    step3(0, 0)
     read_stats(0, 0)
     read_stats(0, 1)
     step3(0, 1)
@@ -368,14 +369,21 @@
 
     step3_in(0, 0)
     lax.fori_loop(0, 4, activate_both, 0)
+    arrived(idf.at[pl.ds(0, 7), :, 0], i2r)
+    for k in range(2):
+        id3(k).start()
     w2_in(0)
     step3_in(0, 1)
     lax.fori_loop(4, 8, activate_both, 0)
     wd_in(0)
     for i in range(2):
-        multiply(0, i, range(8), lambda q: act[q, i], True)
+        multiply(0, i, range(8), True)
         finish(0, i, a[0, qme, i])
         begin(1, i)
+
+    arrived(idf.at[pl.ds(0, 4)], i3r)
+    positions()
+    selection(0, 8)
 
     def layer(l, carry):
         near = [cube_q(CUBE[d]) for d in range(3)]
@@ -400,39 +408,33 @@
         w1_rest(l)
         step3(l, 1)
 
+        for q in mid:
+            activate(l, 0, q)
+        for q in mid:
+            activate(l, 1, q)
+        most = [qme] + near + mid
+
         @pl.when(l == 1)
         def _():
-            arrived(idf.at[pl.ds(0, 7), :, 0], i2r)
-            for k in range(2):
-                id3(k).start()
+            selection(8, 16)
             drain_act(0)
-            drain_stats(0)
             left(seven, i1s)
-
-        @pl.when(l == 2)
-        def _():
-            arrived(idf.at[pl.ds(0, 4)], i3r)
-            positions()
             left(idf.at[pl.ds(0, 7), :, 0], i2s)
+            left(idf.at[pl.ds(0, 4)], i3s)
 
         @pl.when(l >= 2)
         def _():
-            selection((l - 2) * 8, (l - 1) * 8)
             drain_act(l - 1)
-            drain_stats(l - 1)
-
+
+        w2_in(l)
+        drain_stats(l - 1)
         drain_weights(l - 1)
-        for q in mid:
-            activate(l, 0, q)
-        w2_in(l)
-        for q in mid:
-            activate(l, 1, q)
         wd_in(l)
         for i in range(2):
-            multiply(l, i, [qme] + near + mid, lambda q: act[q, i], True)
+            multiply(l, i, most, True)
             step3_in(l, i)
             activate(l, i, cube_q(ALL))
-            multiply(l, i, [cube_q(ALL)], lambda q: act[q, i], False)
+            multiply(l, i, [cube_q(ALL)], False)
             finish(l, i, a[l, qme, i])
 
             @pl.when(l < LAYERS - 1)
@@ -451,7 +453,6 @@
     drain_weights(LAYERS - 1)
     drain_act(LAYERS - 1)
     drain_stats(LAYERS - 1)
-    left(idf.at[pl.ds(0, 4)], i3s)
 
     def place(first, last, groups):
         for m in range(4):
@@ -472,12 +473,14 @@
         arrived(f.at[0, :, 0], fr.at[k])
         out2(k + 1).start()
     place(True, False, [(xh * 2 + core) * 2 + k for k in range(2)])
+    arrived(f.at[pl.ds(0, 2)], fdr.at[0])
+    place(False, False, [(xh * 2 + 1 - core) * 2 + k for k in range(2)])
     for k in range(3, 7):
         arrived(f.at[0, :, 0], fr.at[k])
         out2(k + 1).start()
     place(False, False, [((1 - xh) * 2 + core) * 2 + k for k in range(2)])
-    arrived(f.at[pl.ds(0, 4)], fdr)
-    place(False, True, [(k // 2 * 2 + 1 - core) * 2 + k % 2 for k in range(4)])
+    arrived(f.at[pl.ds(0, 2)], fdr.at[1])
+    place(False, True, [((1 - xh) * 2 + 1 - core) * 2 + k for k in range(2)])
 
     left(f.at[pl.ds(0, 7), :, 0], fs)
     left(f.at[pl.ds(0, 4)], fds)
@@ -525,7 +528,7 @@
             dma,
             dma((7,)),
             dma,
-            dma,
+            dma((2,)),
         ],
         compiler_params=pltpu.CompilerParams(
             collective_id=0, has_side_effects=True, vmem_limit_bytes=60 * 1024 * 1024

time: 96.8 us -> 95.8 us (0.990)
  Pallas kernels: 96 us -> 95 us
    pallas_call x1, Pallas kernels: 96 us -> 95 us  [shards(): pl.pallas_call(kernel, out_shape=pltpu.VMEM((1024, 128), BF16), in_specs=...]
where the time goes in v5:
time: 95.8 us; the launch traced here: 95.7 us
  Pallas kernels  95 us (99%)
    pallas_call x1, Pallas kernels, shards(): pl.pallas_call(kernel, out_shape=pltpu.VMEM((1024, 128), BF16), in_specs=...  95 us

profile of v5, /device:TPU:1, one launch (start us, length us, event | category | flops | bytes accessed | tf_op | source)
XLA Modules:
  0.0 95.7 jit_solution(14211423535891775110)
XLA Ops:
  0.0 95.0 %shard_map.55 = bf16[1024,128]{1,0:T(8,128)(2,1)S(1)} custom-call(bf16[32,4096]{1,0:T(8,128)(2,1)} %rows_in.1, s32[1,32]{1,0:T(1,128)} %bitcast.3, bf16[8,4096]{1,0:T(8,128)(2,1)} %embed_in.1, f32[4,4096]{1,0:T(4,128)} %gain_in.1, bf16[4,4,4,2,128,128]{5,4,3,2,1,0:T(8,128)(2,1)} %bitcast.2), custom_call_target="tpu_custom_call" | custom-call | tf_op jit(solution)/shard_map/pallas_call | solution.py:492
  95.0 0.7 copy.7

commit v6 on v5

--- a/solution.py
+++ b/solution.py
@@ -197,14 +197,17 @@
     def finish(l, i, held):
         new = (held.astype(F32) + acc[i]).astype(BF16)
         a[l + 1, qme, i] = new
-        val = new.astype(F32)
+
+    def tell(l, i):
+        val = a[l, qme, i].astype(F32)
         sq = val * val
         sq = (sq[:, 0:128] + sq[:, 128:256]) + (sq[:, 256:384] + sq[:, 384:512])
         total = jnp.sum(sq, axis=1, keepdims=True)
         line = jnp.sum(jnp.where(eye(), total, 0.0), axis=0, keepdims=True)
-        stat[l + 1, i, qme, 0:1] = line
+        stat[l, i, qme, 0:1] = line
 
     def begin(l, i):
+        tell(l, i)
         for k in range(7):
             stat_copy(l, k, i).start()
         step1(l, i)
@@ -244,14 +247,14 @@
         return remote(src, f.at[g_me, i, b_me], fs, fr.at[k], far_dev(FAR[k]))
 
     def out_begin(i):
+        f[g_me, i, b_me] = a[LAYERS, qme, i, :, cols(slot(0, 0))]
         for k in range(7):
             out1(k, i).start()
-        f[g_me, i, b_me] = a[LAYERS, qme, i, :, cols(slot(0, 0))]
 
     def out2(k):
         fl = ([ME] + FAR)[k]
         g, b = far_at(fl)
-        return both(f.at[g, :, b], fds, fdr.at[k // 4], partner)
+        return both(f.at[g, :, b], fds, fdr.at[max(k // 2 - 1, 0)], partner)
 
     def positions():
         spread = idf[...].reshape(256, 128).astype(F32).astype(BF16)
@@ -372,9 +375,9 @@
     arrived(idf.at[pl.ds(0, 7), :, 0], i2r)
     for k in range(2):
         id3(k).start()
-    w2_in(0)
     step3_in(0, 1)
     lax.fori_loop(4, 8, activate_both, 0)
+    w2_in(0)
     wd_in(0)
     for i in range(2):
         multiply(0, i, range(8), True)
@@ -457,13 +460,15 @@
     def place(first, last, groups):
         for m in range(4):
             lines = slice(m * 256, m * 256 + 256)
-            total = None if first else oacc[lines]
+            total = None
             for at in groups:
                 for k in range(2):
                     part = jnp.dot(
                         pm[at * 2 + k, lines], f[at, k].reshape(256, 128), preferred_element_type=F32
                     )
                     total = part if total is None else total + part
+            if not first:
+                total = total + oacc[lines]
             if last:
                 out_ref[lines] = total.astype(BF16)
             else:
@@ -479,8 +484,10 @@
         arrived(f.at[0, :, 0], fr.at[k])
         out2(k + 1).start()
     place(False, False, [((1 - xh) * 2 + core) * 2 + k for k in range(2)])
-    arrived(f.at[pl.ds(0, 2)], fdr.at[1])
-    place(False, True, [((1 - xh) * 2 + 1 - core) * 2 + k for k in range(2)])
+    arrived(f.at[0], fdr.at[1])
+    place(False, False, [((1 - xh) * 2 + 1 - core) * 2 + zh])
+    arrived(f.at[0], fdr.at[2])
+    place(False, True, [((1 - xh) * 2 + 1 - core) * 2 + 1 - zh])
 
     left(f.at[pl.ds(0, 7), :, 0], fs)
     left(f.at[pl.ds(0, 4)], fds)
@@ -528,7 +535,7 @@
             dma,
             dma((7,)),
             dma,
-            dma((2,)),
+            dma((3,)),
         ],
         compiler_params=pltpu.CompilerParams(
             collective_id=0, has_side_effects=True, vmem_limit_bytes=60 * 1024 * 1024

time: 95.8 us -> 95.4 us (level)
  no operation moved by 1% of the time
where the time goes in v6:
time: 95.4 us; the launch traced here: 95.3 us
  Pallas kernels  94.6 us (99%)
    pallas_call x1, Pallas kernels, shards(): pl.pallas_call(kernel, out_shape=pltpu.VMEM((1024, 128), BF16), in_specs=...  94.6 us

profile of v6, /device:TPU:1, one launch (start us, length us, event | category | flops | bytes accessed | tf_op | source)
XLA Modules:
  0.0 95.3 jit_solution(17653952005028390022)
XLA Ops:
  0.0 94.6 %shard_map.55 = bf16[1024,128]{1,0:T(8,128)(2,1)S(1)} custom-call(bf16[32,4096]{1,0:T(8,128)(2,1)} %rows_in.1, s32[1,32]{1,0:T(1,128)} %bitcast.3, bf16[8,4096]{1,0:T(8,128)(2,1)} %embed_in.1, f32[4,4096]{1,0:T(4,128)} %gain_in.1, bf16[4,4,4,2,128,128]{5,4,3,2,1,0:T(8,128)(2,1)} %bitcast.2), custom_call_target="tpu_custom_call" | custom-call | tf_op jit(solution)/shard_map/pallas_call | solution.py:499
  94.6 0.7 copy.7

commit v7 on v6

--- a/solution.py
+++ b/solution.py
@@ -377,10 +377,14 @@
         id3(k).start()
     step3_in(0, 1)
     lax.fori_loop(4, 8, activate_both, 0)
+    mine = [core * 4 + k for k in range(4)]
+    others = [(1 - core) * 4 + k for k in range(4)]
     w2_in(0)
+    for i in range(2):
+        multiply(0, i, mine, True)
     wd_in(0)
     for i in range(2):
-        multiply(0, i, range(8), True)
+        multiply(0, i, others, False)
         finish(0, i, a[0, qme, i])
         begin(1, i)
 
@@ -415,6 +419,7 @@
             activate(l, 0, q)
         for q in mid:
             activate(l, 1, q)
+
         most = [qme] + near + mid
 
         @pl.when(l == 1)

time: 95.4 us -> 96.5 us (1.012)
  Pallas kernels: 94.6 us -> 95.7 us
    pallas_call x1, Pallas kernels: 94.6 us -> 95.7 us  [shards(): pl.pallas_call(kernel, out_shape=pltpu.VMEM((1024, 128), BF16), in_specs=...]
where the time goes in v7:
time: 96.5 us; the launch traced here: 96.4 us
  Pallas kernels  95.7 us (99%)
    pallas_call x1, Pallas kernels, shards(): pl.pallas_call(kernel, out_shape=pltpu.VMEM((1024, 128), BF16), in_specs=...  95.7 us

profile of v7, /device:TPU:1, one launch (start us, length us, event | category | flops | bytes accessed | tf_op | source)
XLA Modules:
  0.0 96.4 jit_solution(14639824232041780531)
XLA Ops:
  0.0 95.7 %shard_map.55 = bf16[1024,128]{1,0:T(8,128)(2,1)S(1)} custom-call(bf16[32,4096]{1,0:T(8,128)(2,1)} %rows_in.1, s32[1,32]{1,0:T(1,128)} %bitcast.3, bf16[8,4096]{1,0:T(8,128)(2,1)} %embed_in.1, f32[4,4096]{1,0:T(4,128)} %gain_in.1, bf16[4,4,4,2,128,128]{5,4,3,2,1,0:T(8,128)(2,1)} %bitcast.2), custom_call_target="tpu_custom_call" | custom-call | tf_op jit(solution)/shard_map/pallas_call | solution.py:504
  95.7 0.7 copy.7
